TPU v7x, 32 devices: a whole 2x2x4 slice. The times are simulated.
32 devices in a mesh: group: 2 (over y), dp: 4 (over z), tensor: 4 (over x, core).
Axes of the slice: x: 2, y: 2, z: 4, core: 2. Of those that a mesh axis runs over, the one named last changes fastest.
Arguments:
- queries: bfloat16 [32, 4, 8192], P(('group', 'dp')), may hold values from -330 to 330
- keys: bfloat16 [32, 8, 512, 128], P(('group', 'dp'), None, 'tensor'), may hold values from -12 to 12
- values: bfloat16 [32, 8, 512, 128], P(('group', 'dp'), None, 'tensor'), may hold values from -12 to 12
- cached_length: int32 [32], P(('group', 'dp')), may hold values from 2 to 508
- out_weight: bfloat16 [8192, 8192], P('tensor', ('group', 'dp')), may hold values from -0.0625 to 0.0625
Outputs:
- projected: bfloat16 [128, 2, 4096], P(('group', 'tensor'), None, 'dp')
Inputs may be any that keep to these rules, and one draw needn't show every extreme that they name: The keys and values of row r's 4 new tokens sit at positions cached_length[r] to cached_length[r] + 3.
All inputs are finite; a program needn't handle non-finite values.
Results may differ from a plain program's by a relative error of at most 0.018.
Values may be sent and summed in bfloat16 or wider, within the bound.
No kernel may reach another device: no remote copies, remote signals or barrier semaphores. Data moves between devices by JAX's collectives and lax.ppermute only.
A program may use at most 64 MiB of HBM per device.

v0:
```python
import functools
import math

import jax
import jax.numpy as jnp
from jax import lax
from jax.experimental import pallas as pl
from jax.experimental.pallas import tpu as pltpu
from jax.sharding import PartitionSpec as P


F32, BF16 = jnp.float32, jnp.bfloat16
LANES, SUBLANES = 128, 8
MASKED = -1e30
FETCH_FLOPS = 1 << 27


def vmem(shape, dtype):
    return pltpu.VMEM(shape, dtype)


def whole(n):
    return [pl.BlockSpec(memory_space=pltpu.VMEM)] * n


def held(*arrays):
    return [pltpu.with_memory_space_constraint(x, pltpu.VMEM) for x in arrays]


def in_hbm(*arrays):
    return [pltpu.with_memory_space_constraint(x, pltpu.HBM) for x in arrays]


def fetch_kernel(_, w_hbm, w_ref, sem):
    copy = pltpu.make_async_copy(w_hbm, w_ref, sem)
    copy.start()
    copy.wait()


def fetch(after, weight):
    return pl.pallas_call(
        fetch_kernel,
        out_shape=vmem(weight.shape, weight.dtype),
        in_specs=[pl.BlockSpec(memory_space=pltpu.VMEM), pl.BlockSpec(memory_space=pltpu.HBM)],
        out_specs=pl.BlockSpec(memory_space=pltpu.VMEM),
        scratch_shapes=[pltpu.SemaphoreType.DMA],
        cost_estimate=pl.CostEstimate(flops=FETCH_FLOPS, bytes_accessed=weight.size * 2, transcendentals=0),
        compiler_params=pltpu.CompilerParams(vmem_limit_bytes=1 << 20),
        name="fetch",
    )(*held(after), *in_hbm(weight))


def split3(x):
    hi = x.astype(BF16)
    rest = x - hi.astype(F32)
    mid = rest.astype(BF16)
    return hi, mid, (rest - mid.astype(F32)).astype(BF16)


def pack_stats(m, l, heads):
    lane = lax.broadcasted_iota(jnp.int32, m.shape, 1)
    out = jnp.zeros(m.shape, F32)
    for i, part in enumerate(split3(m) + split3(l)):
        term = jnp.where(lane < heads, part.astype(F32), 0.0)
        out = out + (pltpu.roll(term, i * heads, 1) if i else term)
    return out.astype(BF16)


def unpack_stats(packed, heads):
    x = packed.astype(F32)
    lane = lax.broadcasted_iota(jnp.int32, x.shape, 1)

    def term(i):
        return pltpu.roll(x, LANES - i * heads, 1) if i else x

    m = (term(0) + term(1)) + term(2)
    l = (term(3) + term(4)) + term(5)
    return jnp.where(lane < heads, m, 0.0), jnp.where(lane < heads, l, 0.0)


def attention_kernel(heads, join, len_hbm, q_hbm, k_hbm, v_hbm, send_ref, acc_ref, stat_ref, len_scr, q_scr, k_scr, v_scr, f_scr, o_scr, s_scr, sems):
    rows, steps, model = q_hbm.shape
    kv_heads, cache, dim = k_hbm.shape[1:]
    q_heads = model // dim
    per_kv = q_heads // kv_heads
    tensor, width, parts, span = q_heads // heads, heads * dim, heads // join, k_scr.shape[2]
    me = lax.axis_index("tensor")
    order = list(range(1, tensor, 2)) + list(range(0, tensor, 2))
    copies = []
    for chunk in range(tensor):
        owner = me ^ chunk
        kv = owner * heads // per_kv
        copies.append([
            pltpu.make_async_copy(q_hbm.at[:, :, pl.ds(pl.multiple_of(owner * width, width), width)], q_scr.at[chunk], sems.at[0, chunk]),
            pltpu.make_async_copy(k_hbm.at[:, pl.ds(kv, span)], k_scr.at[chunk], sems.at[1, chunk]),
            pltpu.make_async_copy(v_hbm.at[:, pl.ds(kv, span)], v_scr.at[chunk], sems.at[2, chunk]),
        ])
    limits = pltpu.make_async_copy(len_hbm, len_scr, sems.at[3, 0])
    limits.start()
    for chunk in order:
        for copy in copies[chunk]:
            copy.start()
    limits.wait()
    scale = 1.0 / math.sqrt(dim)
    m_rows = join * steps
    row = lax.broadcasted_iota(jnp.int32, (m_rows, cache), 0)
    position = me * cache + lax.broadcasted_iota(jnp.int32, (m_rows, cache), 1) - row % steps
    lane = lax.broadcasted_iota(jnp.int32, (m_rows, LANES), 1)
    srow = lax.broadcasted_iota(jnp.int32, (m_rows, LANES), 0)
    allowed = [position < len_scr[r] + 1 for r in range(rows)]
    for chunk in order:
        units = [(part, r) for part in range(parts) for r in range(rows)]
        copies[chunk][0].wait()
        for u, (part, r) in enumerate(units):
            for j in range(join):
                f_scr[chunk, u, pl.ds(j * steps, steps), :] = q_scr[chunk, r, :, pl.ds((part * join + j) * dim, dim)].astype(F32)
        copies[chunk][1].wait()
        s = [
            lax.dot_general(
                f_scr[chunk, u].astype(BF16), k_scr[chunk, r, part * span // parts],
                (((1,), (1,)), ((), ())), preferred_element_type=F32,
            )
            for u, (part, r) in enumerate(units)
        ]
        s = [jnp.where(allowed[r], x * scale, MASKED) for x, (_, r) in zip(s, units)]
        m = [jnp.max(x, axis=1, keepdims=True) for x in s]
        p = [jnp.where(allowed[r], jnp.exp(x - y), 0.0) for x, y, (_, r) in zip(s, m, units)]
        l = [jnp.sum(x, axis=1, keepdims=True) for x in p]
        copies[chunk][2].wait()
        o = [
            jnp.dot(x.astype(BF16), v_scr[chunk, r, part * span // parts], preferred_element_type=F32)
            for x, (part, r) in zip(p, units)
        ]
        for x, (part, r) in zip(o, units):
            for j in range(join):
                o_scr[chunk, pl.ds(r * steps, steps), pl.ds((part * join + j) * dim, dim)] = x[j * steps : (j + 1) * steps]
        for i, stat in enumerate((m, l)):
            for r in range(rows):
                total = 0.0
                for x, (part, at) in zip(stat, units):
                    if at == r:
                        x = jnp.where(lane == part * join + srow // steps, x, 0.0)
                        for b in range(0, m_rows, SUBLANES):
                            total = total + x[b : b + SUBLANES]
                shift = steps
                while shift < SUBLANES:
                    total = total + pltpu.roll(total, shift, 0)
                    shift *= 2
                s_scr[chunk, i, pl.ds(r * steps, steps), :] = total[:steps]
        half = chunk // 2
        if chunk % 2:
            send_ref[half, :, pl.ds(0, width)] = o_scr[chunk].astype(BF16)
            send_ref[half, :, pl.ds(width, LANES)] = pack_stats(s_scr[chunk, 0], s_scr[chunk, 1], heads)
        else:
            acc_ref[half] = o_scr[chunk]
            stat_ref[half] = s_scr[chunk]


def attention(queries, keys, values, lengths, tensor):
    rows, steps, model = queries.shape
    kv_heads, cache, dim = keys.shape[1:]
    q_heads = model // dim
    heads = q_heads // tensor
    per_kv = q_heads // kv_heads
    join, span = min(heads, per_kv), max(1, heads // per_kv)
    width, tokens, halves = heads * dim, rows * steps, tensor // 2
    return pl.pallas_call(
        functools.partial(attention_kernel, heads, join),
        out_shape=(
            vmem((halves, tokens, width + LANES), BF16),
            vmem((halves, tokens, width), F32),
            vmem((halves, 2, tokens, LANES), F32),
        ),
        in_specs=[pl.BlockSpec(memory_space=pltpu.HBM)] * 4,
        out_specs=whole(3),
        scratch_shapes=[
            pltpu.SMEM((rows,), jnp.int32),
            pltpu.VMEM((tensor, rows, steps, width), BF16),
            pltpu.VMEM((tensor, rows, span, cache, dim), BF16),
            pltpu.VMEM((tensor, rows, span, cache, dim), BF16),
            pltpu.VMEM((tensor, rows * heads // join, join * steps, dim), F32),
            pltpu.VMEM((tensor, tokens, width), F32),
            pltpu.VMEM((tensor, 2, tokens, LANES), F32),
            pltpu.SemaphoreType.DMA((4, tensor)),
        ],
        compiler_params=pltpu.CompilerParams(vmem_limit_bytes=16 << 20),
        name="attention",
    )(*in_hbm(lengths, queries, keys, values))


def merged(acc, m, l, received, heads):
    width = acc.shape[1]
    dim = width // heads
    m2, l2 = unpack_stats(received[:, width:], heads)
    top = jnp.maximum(m, m2)
    e1, e2 = jnp.exp(m - top), jnp.exp(m2 - top)
    columns = [
        e1[:, i : i + 1] * acc[:, i * dim : (i + 1) * dim]
        + e2[:, i : i + 1] * received[:, i * dim : (i + 1) * dim].astype(F32)
        for i in range(heads)
    ]
    return columns, top, e1 * l + e2 * l2


def core_merge_kernel(heads, acc_ref, stat_ref, recv_ref, send_ref, own_ref, own_stat_ref):
    width = acc_ref.shape[2]
    dim = width // heads
    for k in range(acc_ref.shape[0]):
        columns, m, l = merged(acc_ref[k], stat_ref[k, 0], stat_ref[k, 1], recv_ref[k], heads)
        for i, c in enumerate(columns):
            if k:
                send_ref[k - 1, :, pl.ds(i * dim, dim)] = c.astype(BF16)
            else:
                own_ref[:, pl.ds(i * dim, dim)] = c
        if k:
            send_ref[k - 1, :, pl.ds(width, LANES)] = pack_stats(m, l, heads)
        else:
            own_stat_ref[0] = m
            own_stat_ref[1] = l


def core_merge(acc, stat, received, heads):
    halves, tokens, width = acc.shape
    return pl.pallas_call(
        functools.partial(core_merge_kernel, heads),
        out_shape=(
            vmem((halves - 1, tokens, width + LANES), BF16),
            vmem((tokens, width), F32),
            vmem((2, tokens, LANES), F32),
        ),
        in_specs=whole(3),
        out_specs=whole(3),
        compiler_params=pltpu.CompilerParams(vmem_limit_bytes=8 << 20),
        name="core_merge",
    )(*held(acc, stat, received))


def final_merge_kernel(heads, n, own_ref, stat_ref, *refs):
    recv, out_ref = refs[:n], refs[n]
    width = own_ref.shape[1]
    dim = width // heads
    acc, m, l = own_ref[...], stat_ref[0], stat_ref[1]
    for r in recv:
        columns, m, l = merged(acc, m, l, r[...], heads)
        acc = jnp.concatenate(columns, axis=1)
    inverse = 1.0 / l
    for i in range(heads):
        out_ref[:, pl.ds(i * dim, dim)] = (
            acc[:, i * dim : (i + 1) * dim] * inverse[:, i : i + 1]
        ).astype(BF16)


def final_merge(own, stat, received, heads):
    return pl.pallas_call(
        functools.partial(final_merge_kernel, heads, len(received)),
        out_shape=vmem(own.shape, BF16),
        in_specs=whole(2 + len(received)),
        out_specs=pl.BlockSpec(memory_space=pltpu.VMEM),
        compiler_params=pltpu.CompilerParams(vmem_limit_bytes=8 << 20),
        name="final_merge",
    )(*held(own, stat, *received))


def project_kernel(groups, dps, halves, *refs):
    blocks, w_ref = refs[: groups * dps], refs[groups * dps]
    send_ref, keep_ref, lhs = refs[groups * dps + 1 :]
    tokens = blocks[0].shape[0]
    twist = lax.axis_index("dp") ^ lax.axis_index("tensor")
    for kg in range(groups):
        for kd in range(dps):
            at = kg * dps + (twist ^ kd)
            lhs[pl.ds(pl.multiple_of(at * tokens, tokens), tokens), :] = blocks[kg * dps + kd][...]
    out = jnp.dot(lhs[...], w_ref[...], preferred_element_type=F32)
    for kg in range(groups):
        for kt in range(2 * halves):
            piece = out[(kg * dps + kt) * tokens : (kg * dps + kt + 1) * tokens]
            if kt % 2:
                send_ref[kg, kt // 2] = piece.astype(BF16)
            else:
                keep_ref[kg, kt // 2] = piece


def project(blocks, weight, groups, dps, halves):
    tokens, width = blocks[0].shape
    columns = weight.shape[1]
    shape = (groups, halves, tokens, columns)
    return pl.pallas_call(
        functools.partial(project_kernel, groups, dps, halves),
        out_shape=(vmem(shape, BF16), vmem(shape, F32)),
        in_specs=whole(len(blocks) + 1),
        out_specs=whole(2),
        scratch_shapes=[pltpu.VMEM((groups * dps * tokens, width), BF16)],
        compiler_params=pltpu.CompilerParams(vmem_limit_bytes=16 << 20),
        name="project",
    )(*held(*blocks, weight))


def swap(x, axes, n, k):
    return lax.ppermute(x, axes, [(i, i ^ k) for i in range(n)])


def on_device(queries, keys, values, cached_length, out_weight):
    _, _, model = queries.shape
    q_heads = model // keys.shape[3]
    tensor, groups, dps = lax.axis_size("tensor"), lax.axis_size("group"), lax.axis_size("dp")
    halves, heads = tensor // 2, q_heads // tensor

    send, acc, stat = attention(queries, keys, values, cached_length, tensor)
    send, own, stat = core_merge(acc, stat, swap(send, "tensor", tensor, 1), heads)
    weight = fetch(stat, out_weight)
    arrived = [swap(send[k - 1], "tensor", tensor, 2 * k) for k in range(1, halves)]
    attended = final_merge(own, stat, arrived, heads)

    line = [attended]
    for k in range(1, dps):
        line.append(swap(attended, "dp", dps, k))
    blocks = list(line)
    for kg in range(1, groups):
        for b in line:
            blocks.append(swap(b, "group", groups, kg))
    send, keep = project(blocks, weight, groups, dps, halves)

    both = keep + swap(send, "tensor", tensor, 1).astype(F32)
    plane, n = ("group", "tensor"), groups * tensor
    sums = []
    for kg in range(groups):
        total = both[0, 0] if kg == 0 else 0.0
        for kx in range(halves):
            if kg or kx:
                total = total + swap(both[kg, kx].astype(BF16), plane, n, kg * tensor + 2 * kx).astype(F32)
        sums.append(total)
    me = lax.axis_index("group")
    placed = []
    for g in range(groups):
        kept = sums[0]
        for kg in range(1, groups):
            kept = jnp.where(me ^ kg == g, sums[kg], kept)
        placed.append(kept)
    return jnp.stack(placed, axis=1).astype(BF16)


def solution(mesh):
    in_specs = (
        P(("group", "dp"), None, None),
        P(("group", "dp"), None, "tensor", None),
        P(("group", "dp"), None, "tensor", None),
        P(("group", "dp")),
        P("tensor", ("group", "dp")),
    )
    out_specs = P(("group", "tensor"), None, "dp")
    return jax.shard_map(
        on_device, mesh=mesh, in_specs=in_specs, out_specs=out_specs, check_vma=False
    )
```

profile of v0, /device:TPU:0, one launch (start us, length us, event | category | flops | bytes accessed | tf_op | source)
XLA Modules:
  0.0 36.1 jit_solution(12743185954262909829)
XLA Ops:
  0.0 3.6 %attention.1 = (bf16[2,16,2176]{2,1,0:T(8,128)(2,1)S(1)}, f32[2,16,2048]{2,1,0:T(8,128)S(1)}, f32[2,2,16,128]{3,2,1,0:T(8,128)S(1)}) custom-call(s32[4]{0:T(128)} %len_hbm.1, bf16[4,4,8192]{2,1,0:T(4,128)(2,1)} %q_hbm.1, bf16[4,8,128,128]{3,2,1,0:T(8,128)(2,1)} %k_hbm.1, bf16[4,8,128,128]{3,2,1,0:T(8,128)(2,1)} %v_hbm.1), custom_call_target="tpu_custom_call" | custom-call | tf_op jit(solution)/shard_map/attention/pallas_call | solution.py:167
  3.7 0.6 %collective-permute-start = (bf16[2,16,2176]{2,1,0:T(8,128)(2,1)S(1)}, bf16[2,16,2176]{2,1,0:T(8,128)(2,1)S(1)}, u32[]{:S(2)}, u32[]{:S(2)}) collective-permute-start(bf16[2,16,2176]{2,1,0:T(8,128)(2,1)S(1)} %get-tuple-element.15), channel_id=1, source_target_pairs={{0,1},{1,0},{2,3},{3,2},{4,5},{5,4},{6,7},{7,6},{8,9},{9,8},{10,11... | collective-permute-start | bytes 417800 | tf_op jit(solution)/shard_map/ppermute | solution.py:299
  4.2 1.0 %collective-permute-done.recv_ref = bf16[2,16,2176]{2,1,0:T(8,128)(2,1)S(1)} collective-permute-done((bf16[2,16,2176]{2,1,0:T(8,128)(2,1)S(1)}, bf16[2,16,2176]{2,1,0:T(8,128)(2,1)S(1)}, u32[]{:S(2)}, u32[]{:S(2)}) %collective-permute-start) | collective-permute-done | bytes 139296 | tf_op jit(solution)/shard_map/ppermute | solution.py:299
  5.2 0.4 %core_merge.1 = (bf16[1,16,2176]{2,1,0:T(8,128)(2,1)S(1)}, f32[16,2048]{1,0:T(8,128)S(1)}, f32[2,16,128]{2,1,0:T(8,128)S(1)}) custom-call(f32[2,16,2048]{2,1,0:T(8,128)S(1)} %get-tuple-element.13.acc_ref, f32[2,2,16,128]{3,2,1,0:T(8,128)S(1)} %get-tuple-element.14.stat_ref, bf16[2,16,2176]{2,1,0:T(8,128)(2,1)S(1)} %collective-permute-done.recv_ref), custom_call_target="tpu_custom_call" | custom-call | tf_op jit(solution)/shard_map/core_merge/pallas_call | solution.py:224
  5.6 2.9 %collective-permute-start.1 = (bf16[16,2176]{1,0:T(8,128)(2,1)S(1)}, bf16[16,2176]{1,0:T(8,128)(2,1)S(1)}, u32[]{:S(2)}, u32[]{:S(2)}) collective-permute-start(bf16[16,2176]{1,0:T(8,128)(2,1)S(1)} %bitcast.23), channel_id=1, source_target_pairs={{0,2},{1,3},{2,0},{3,1},{4,6},{5,7},{6,4},{7,5},{8,10},{9,11},{10,... | collective-permute-start | bytes 208904 | tf_op jit(solution)/shard_map/ppermute | solution.py:299
  8.5 2.5 %collective-permute-done.1.refs_0_ = bf16[16,2176]{1,0:T(8,128)(2,1)S(1)} collective-permute-done((bf16[16,2176]{1,0:T(8,128)(2,1)S(1)}, bf16[16,2176]{1,0:T(8,128)(2,1)S(1)}, u32[]{:S(2)}, u32[]{:S(2)}) %collective-permute-start.1) | collective-permute-done | bytes 69664 | tf_op jit(solution)/shard_map/ppermute | solution.py:299
  11.0 0.3 final_merge.1.refs_0_
  11.3 2.0 %collective-permute-start.2 = (bf16[16,2048]{1,0:T(8,128)(2,1)S(1)}, bf16[16,2048]{1,0:T(8,128)(2,1)S(1)}, u32[]{:S(2)}, u32[]{:S(2)}) collective-permute-start(bf16[16,2048]{1,0:T(8,128)(2,1)S(1)} %final_merge.1.refs_0_), channel_id=1, source_target_pairs={{0,4},{4,0},{8,12},{12,8},{1,5},{5,1},{9,13},{13,9},{2,6},{6,2},{1... | collective-permute-start | bytes 196616 | tf_op jit(solution)/shard_map/ppermute | solution.py:299
  13.3 2.6 %collective-permute-start.3 = (bf16[16,2048]{1,0:T(8,128)(2,1)S(1)}, bf16[16,2048]{1,0:T(8,128)(2,1)S(1)}, u32[]{:S(2)}, u32[]{:S(2)}) collective-permute-start(bf16[16,2048]{1,0:T(8,128)(2,1)S(1)} %final_merge.1.refs_0_), channel_id=1, source_target_pairs={{0,8},{4,12},{8,0},{12,4},{1,9},{5,13},{9,1},{13,5},{2,10},{6,14},... | collective-permute-start | bytes 196616 | tf_op jit(solution)/shard_map/ppermute | solution.py:299
  15.9 0.0 collective-permute-start.4
  15.9 1.7 %collective-permute-start.5 = (bf16[16,2048]{1,0:T(8,128)(2,1)S(1)}, bf16[16,2048]{1,0:T(8,128)(2,1)S(1)}, u32[]{:S(2)}, u32[]{:S(2)}) collective-permute-start(bf16[16,2048]{1,0:T(8,128)(2,1)S(1)} %final_merge.1.refs_0_), channel_id=1, source_target_pairs={{0,16},{16,0},{1,17},{17,1},{2,18},{18,2},{3,19},{19,3},{4,20},{20... | collective-permute-start | bytes 196616 | tf_op jit(solution)/shard_map/ppermute | solution.py:299
  17.6 0.0 collective-permute-done.2.refs_1_
  17.6 0.5 %collective-permute-start.6 = (bf16[16,2048]{1,0:T(8,128)(2,1)S(1)}, bf16[16,2048]{1,0:T(8,128)(2,1)S(1)}, u32[]{:S(2)}, u32[]{:S(2)}) collective-permute-start(bf16[16,2048]{1,0:T(8,128)(2,1)S(1)} %collective-permute-done.2.refs_1_), channel_id=1, source_target_pairs={{0,16},{16,0},{1,17},{17,1},{2,18},{18,2},{3,19},{19,3},{4,20},{20... | collective-permute-start | bytes 196616 | tf_op jit(solution)/shard_map/ppermute | solution.py:299
  18.1 1.7 %collective-permute-done.3.refs_2_ = bf16[16,2048]{1,0:T(8,128)(2,1)S(1)} collective-permute-done((bf16[16,2048]{1,0:T(8,128)(2,1)S(1)}, bf16[16,2048]{1,0:T(8,128)(2,1)S(1)}, u32[]{:S(2)}, u32[]{:S(2)}) %collective-permute-start.3) | collective-permute-done | bytes 65568 | tf_op jit(solution)/shard_map/ppermute | solution.py:299
  19.9 1.5 %collective-permute-start.7 = (bf16[16,2048]{1,0:T(8,128)(2,1)S(1)}, bf16[16,2048]{1,0:T(8,128)(2,1)S(1)}, u32[]{:S(2)}, u32[]{:S(2)}) collective-permute-start(bf16[16,2048]{1,0:T(8,128)(2,1)S(1)} %collective-permute-done.3.refs_2_), channel_id=1, source_target_pairs={{0,16},{16,0},{1,17},{17,1},{2,18},{18,2},{3,19},{19,3},{4,20},{20... | collective-permute-start | bytes 196616 | tf_op jit(solution)/shard_map/ppermute | solution.py:299
  21.4 0.6 %collective-permute-done.4.refs_3_ = bf16[16,2048]{1,0:T(8,128)(2,1)S(1)} collective-permute-done((bf16[16,2048]{1,0:T(8,128)(2,1)S(1)}, bf16[16,2048]{1,0:T(8,128)(2,1)S(1)}, u32[]{:S(2)}, u32[]{:S(2)}) %collective-permute-start.4) | collective-permute-done | bytes 65568 | tf_op jit(solution)/shard_map/ppermute | solution.py:299
  21.9 1.5 %collective-permute-start.8 = (bf16[16,2048]{1,0:T(8,128)(2,1)S(1)}, bf16[16,2048]{1,0:T(8,128)(2,1)S(1)}, u32[]{:S(2)}, u32[]{:S(2)}) collective-permute-start(bf16[16,2048]{1,0:T(8,128)(2,1)S(1)} %collective-permute-done.4.refs_3_), channel_id=1, source_target_pairs={{0,16},{16,0},{1,17},{17,1},{2,18},{18,2},{3,19},{19,3},{4,20},{20... | collective-permute-start | bytes 196616 | tf_op jit(solution)/shard_map/ppermute | solution.py:299
  23.5 2.2 %fetch.1.refs_8_ = bf16[2048,1024]{1,0:T(8,128)(2,1)S(1)} custom-call(f32[2,16,128]{2,1,0:T(8,128)S(1)} %get-tuple-element.17.stat_ref._, bf16[2048,1024]{1,0:T(8,128)(2,1)} %w_hbm.1), custom_call_target="tpu_custom_call" | custom-call | flops 134217728 | bytes 4194304 | tf_op jit(solution)/shard_map/fetch/pallas_call | solution.py:41
  25.7 0.0 collective-permute-done.5.refs_4_
  25.7 0.0 collective-permute-done.6.refs_5_
  25.7 0.0 collective-permute-done.7.refs_6_
  25.7 0.5 %collective-permute-done.8.refs_7_ = bf16[16,2048]{1,0:T(8,128)(2,1)S(1)} collective-permute-done((bf16[16,2048]{1,0:T(8,128)(2,1)S(1)}, bf16[16,2048]{1,0:T(8,128)(2,1)S(1)}, u32[]{:S(2)}, u32[]{:S(2)}) %collective-permute-start.8) | collective-permute-done | bytes 65568 | tf_op jit(solution)/shard_map/ppermute | solution.py:299
  26.2 0.7 %project.1 = (bf16[2,2,16,1024]{3,2,1,0:T(8,128)(2,1)S(1)}, f32[2,2,16,1024]{3,2,1,0:T(8,128)S(1)}) custom-call(bf16[16,2048]{1,0:T(8,128)(2,1)S(1)} %final_merge.1.refs_0_, bf16[16,2048]{1,0:T(8,128)(2,1)S(1)} %collective-permute-done.2.refs_1_, bf16[16,2048]{1,0:T(8,128)(2,1)S(1)} %collective-permute-done.3.refs_2_, ...), custom_call_target="tpu_custom_call" | custom-call | tf_op jit(solution)/shard_map/project/pallas_call | solution.py:287
  26.9 0.1 collective-permute-start.9
  27.0 1.3 %collective-permute-done.9 = bf16[2,2,16,1024]{3,2,1,0:T(8,128)(2,1)S(1)} collective-permute-done((bf16[2,2,16,1024]{3,2,1,0:T(8,128)(2,1)S(1)}, bf16[2,2,16,1024]{3,2,1,0:T(8,128)(2,1)S(1)}, u32[]{:S(2)}, u32[]{:S(2)}) %collective-permute-start.9) | collective-permute-done | bytes 131104 | tf_op jit(solution)/shard_map/ppermute | solution.py:299
  28.4 1.6 %collective-permute-start.10 = (bf16[16,1024]{1,0:T(8,128)(2,1)S(1)}, bf16[16,1024]{1,0:T(8,128)(2,1)S(1)}, u32[]{:S(2)}, u32[]{:S(2)}) collective-permute-start(bf16[16,1024]{1,0:T(8,128)(2,1)S(1)} %get-tuple-element.25), channel_id=1, source_target_pairs={{0,16},{1,17},{2,18},{3,19},{16,0},{17,1},{18,2},{19,3},{4,20},{5,... | collective-permute-start | bytes 98312 | tf_op jit(solution)/shard_map/ppermute | solution.py:299
  30.0 1.4 %collective-permute-start.11 = (bf16[16,1024]{1,0:T(8,128)(2,1)S(1)}, bf16[16,1024]{1,0:T(8,128)(2,1)S(1)}, u32[]{:S(2)}, u32[]{:S(2)}) collective-permute-start(bf16[16,1024]{1,0:T(8,128)(2,1)S(1)} %get-tuple-element.27), channel_id=1, source_target_pairs={{0,18},{1,19},{2,16},{3,17},{16,2},{17,3},{18,0},{19,1},{4,22},{5,... | collective-permute-start | bytes 98312 | tf_op jit(solution)/shard_map/ppermute | solution.py:299
  31.4 0.5 %collective-permute-start.12 = (bf16[16,1024]{1,0:T(8,128)(2,1)S(1)}, bf16[16,1024]{1,0:T(8,128)(2,1)S(1)}, u32[]{:S(2)}, u32[]{:S(2)}) collective-permute-start(bf16[16,1024]{1,0:T(8,128)(2,1)S(1)} %get-tuple-element.26), channel_id=1, source_target_pairs={{0,2},{1,3},{2,0},{3,1},{16,18},{17,19},{18,16},{19,17},{4,6},{5,7... | collective-permute-start | bytes 98312 | tf_op jit(solution)/shard_map/ppermute | solution.py:299
  32.0 0.4 %collective-permute-done.10 = bf16[16,1024]{1,0:T(8,128)(2,1)S(1)} collective-permute-done((bf16[16,1024]{1,0:T(8,128)(2,1)S(1)}, bf16[16,1024]{1,0:T(8,128)(2,1)S(1)}, u32[]{:S(2)}, u32[]{:S(2)}) %collective-permute-start.10) | collective-permute-done | bytes 32800 | tf_op jit(solution)/shard_map/ppermute | solution.py:299
  32.4 2.7 %collective-permute-done.11 = bf16[16,1024]{1,0:T(8,128)(2,1)S(1)} collective-permute-done((bf16[16,1024]{1,0:T(8,128)(2,1)S(1)}, bf16[16,1024]{1,0:T(8,128)(2,1)S(1)}, u32[]{:S(2)}, u32[]{:S(2)}) %collective-permute-start.11) | collective-permute-done | bytes 32800 | tf_op jit(solution)/shard_map/ppermute | solution.py:299
  35.1 0.3 collective-permute-done.12
  35.4 0.7 %copy.6 = bf16[16,2,1024]{2,1,0:T(2,128)(2,1)} copy(bf16[16,2,1024]{2,0,1:T(8,128)(2,1)S(1)} %pad_maximum_fusion) | data formatting | bytes 131072 | tf_op jit(solution)/shard_map/stack | solution.py:339
  (4 shorter events, 0.1 us)
Async XLA Ops:
  3.7 1.6 %collective-permute-start = (bf16[2,16,2176]{2,1,0:T(8,128)(2,1)S(1)}, bf16[2,16,2176]{2,1,0:T(8,128)(2,1)S(1)}, u32[]{:S(2)}, u32[]{:S(2)}) collective-permute-start(bf16[2,16,2176]{2,1,0:T(8,128)(2,1)S(1)} %get-tuple-element.15), channel_id=1, source_target_pairs={{0,1},{1,0},{2,3},{3,2},{4,5},{5,4},{6,7},{7,6},{8,9},{9,8},{10,11... | collective-permute-start | bytes 417800 | tf_op jit(solution)/shard_map/ppermute | solution.py:299
  5.6 5.4 %collective-permute-start.1 = (bf16[16,2176]{1,0:T(8,128)(2,1)S(1)}, bf16[16,2176]{1,0:T(8,128)(2,1)S(1)}, u32[]{:S(2)}, u32[]{:S(2)}) collective-permute-start(bf16[16,2176]{1,0:T(8,128)(2,1)S(1)} %bitcast.23), channel_id=1, source_target_pairs={{0,2},{1,3},{2,0},{3,1},{4,6},{5,7},{6,4},{7,5},{8,10},{9,11},{10,... | collective-permute-start | bytes 208904 | tf_op jit(solution)/shard_map/ppermute | solution.py:299
  11.3 6.3 %collective-permute-start.2 = (bf16[16,2048]{1,0:T(8,128)(2,1)S(1)}, bf16[16,2048]{1,0:T(8,128)(2,1)S(1)}, u32[]{:S(2)}, u32[]{:S(2)}) collective-permute-start(bf16[16,2048]{1,0:T(8,128)(2,1)S(1)} %final_merge.1.refs_0_), channel_id=1, source_target_pairs={{0,4},{4,0},{8,12},{12,8},{1,5},{5,1},{9,13},{13,9},{2,6},{6,2},{1... | collective-permute-start | bytes 196616 | tf_op jit(solution)/shard_map/ppermute | solution.py:299
  13.3 6.6 %collective-permute-start.3 = (bf16[16,2048]{1,0:T(8,128)(2,1)S(1)}, bf16[16,2048]{1,0:T(8,128)(2,1)S(1)}, u32[]{:S(2)}, u32[]{:S(2)}) collective-permute-start(bf16[16,2048]{1,0:T(8,128)(2,1)S(1)} %final_merge.1.refs_0_), channel_id=1, source_target_pairs={{0,8},{4,12},{8,0},{12,4},{1,9},{5,13},{9,1},{13,5},{2,10},{6,14},... | collective-permute-start | bytes 196616 | tf_op jit(solution)/shard_map/ppermute | solution.py:299
  15.9 6.1 %collective-permute-start.4 = (bf16[16,2048]{1,0:T(8,128)(2,1)S(1)}, bf16[16,2048]{1,0:T(8,128)(2,1)S(1)}, u32[]{:S(2)}, u32[]{:S(2)}) collective-permute-start(bf16[16,2048]{1,0:T(8,128)(2,1)S(1)} %final_merge.1.refs_0_), channel_id=1, source_target_pairs={{0,12},{4,8},{8,4},{12,0},{1,13},{5,9},{9,5},{13,1},{2,14},{6,10},... | collective-permute-start | bytes 196616 | tf_op jit(solution)/shard_map/ppermute | solution.py:299
  15.9 9.8 %collective-permute-start.5 = (bf16[16,2048]{1,0:T(8,128)(2,1)S(1)}, bf16[16,2048]{1,0:T(8,128)(2,1)S(1)}, u32[]{:S(2)}, u32[]{:S(2)}) collective-permute-start(bf16[16,2048]{1,0:T(8,128)(2,1)S(1)} %final_merge.1.refs_0_), channel_id=1, source_target_pairs={{0,16},{16,0},{1,17},{17,1},{2,18},{18,2},{3,19},{19,3},{4,20},{20... | collective-permute-start | bytes 196616 | tf_op jit(solution)/shard_map/ppermute | solution.py:299
  17.6 8.1 %collective-permute-start.6 = (bf16[16,2048]{1,0:T(8,128)(2,1)S(1)}, bf16[16,2048]{1,0:T(8,128)(2,1)S(1)}, u32[]{:S(2)}, u32[]{:S(2)}) collective-permute-start(bf16[16,2048]{1,0:T(8,128)(2,1)S(1)} %collective-permute-done.2.refs_1_), channel_id=1, source_target_pairs={{0,16},{16,0},{1,17},{17,1},{2,18},{18,2},{3,19},{19,3},{4,20},{20... | collective-permute-start | bytes 196616 | tf_op jit(solution)/shard_map/ppermute | solution.py:299
  19.9 5.8 %collective-permute-start.7 = (bf16[16,2048]{1,0:T(8,128)(2,1)S(1)}, bf16[16,2048]{1,0:T(8,128)(2,1)S(1)}, u32[]{:S(2)}, u32[]{:S(2)}) collective-permute-start(bf16[16,2048]{1,0:T(8,128)(2,1)S(1)} %collective-permute-done.3.refs_2_), channel_id=1, source_target_pairs={{0,16},{16,0},{1,17},{17,1},{2,18},{18,2},{3,19},{19,3},{4,20},{20... | collective-permute-start | bytes 196616 | tf_op jit(solution)/shard_map/ppermute | solution.py:299
  21.9 4.3 %collective-permute-start.8 = (bf16[16,2048]{1,0:T(8,128)(2,1)S(1)}, bf16[16,2048]{1,0:T(8,128)(2,1)S(1)}, u32[]{:S(2)}, u32[]{:S(2)}) collective-permute-start(bf16[16,2048]{1,0:T(8,128)(2,1)S(1)} %collective-permute-done.4.refs_3_), channel_id=1, source_target_pairs={{0,16},{16,0},{1,17},{17,1},{2,18},{18,2},{3,19},{19,3},{4,20},{20... | collective-permute-start | bytes 196616 | tf_op jit(solution)/shard_map/ppermute | solution.py:299
  26.9 1.4 %collective-permute-start.9 = (bf16[2,2,16,1024]{3,2,1,0:T(8,128)(2,1)S(1)}, bf16[2,2,16,1024]{3,2,1,0:T(8,128)(2,1)S(1)}, u32[]{:S(2)}, u32[]{:S(2)}) collective-permute-start(bf16[2,2,16,1024]{3,2,1,0:T(8,128)(2,1)S(1)} %get-tuple-element.20), channel_id=1, source_target_pairs={{0,1},{1,0},{2,3},{3,2},{4,5},{5,4},{6,7},{7,6},{8,9},{9,8},{10,11... | collective-permute-start | bytes 393224 | tf_op jit(solution)/shard_map/ppermute | solution.py:299
  28.4 4.0 %collective-permute-start.10 = (bf16[16,1024]{1,0:T(8,128)(2,1)S(1)}, bf16[16,1024]{1,0:T(8,128)(2,1)S(1)}, u32[]{:S(2)}, u32[]{:S(2)}) collective-permute-start(bf16[16,1024]{1,0:T(8,128)(2,1)S(1)} %get-tuple-element.25), channel_id=1, source_target_pairs={{0,16},{1,17},{2,18},{3,19},{16,0},{17,1},{18,2},{19,3},{4,20},{5,... | collective-permute-start | bytes 98312 | tf_op jit(solution)/shard_map/ppermute | solution.py:299
  30.0 5.1 %collective-permute-start.11 = (bf16[16,1024]{1,0:T(8,128)(2,1)S(1)}, bf16[16,1024]{1,0:T(8,128)(2,1)S(1)}, u32[]{:S(2)}, u32[]{:S(2)}) collective-permute-start(bf16[16,1024]{1,0:T(8,128)(2,1)S(1)} %get-tuple-element.27), channel_id=1, source_target_pairs={{0,18},{1,19},{2,16},{3,17},{16,2},{17,3},{18,0},{19,1},{4,22},{5,... | collective-permute-start | bytes 98312 | tf_op jit(solution)/shard_map/ppermute | solution.py:299
  31.4 3.9 %collective-permute-start.12 = (bf16[16,1024]{1,0:T(8,128)(2,1)S(1)}, bf16[16,1024]{1,0:T(8,128)(2,1)S(1)}, u32[]{:S(2)}, u32[]{:S(2)}) collective-permute-start(bf16[16,1024]{1,0:T(8,128)(2,1)S(1)} %get-tuple-element.26), channel_id=1, source_target_pairs={{0,2},{1,3},{2,0},{3,1},{16,18},{17,19},{18,16},{19,17},{4,6},{5,7... | collective-permute-start | bytes 98312 | tf_op jit(solution)/shard_map/ppermute | solution.py:299
where the time goes:
time: 36.3 us; the launch traced here: 36.1 us
  starting transfers between devices  16.9 us (47%)
  waiting for transfers between devices  11 us (30%)
  Pallas kernels  7.28 us (20%)
  local copies, waits for them, and re-layouts  0.71 us (2%)
    ppermute x13, starting transfers between devices, swap(): return lax.ppermute(x, axes, [(i, i ^ k) for i in range(n)])  16.9 us
    ppermute x13, waiting for transfers between devices, swap(): return lax.ppermute(x, axes, [(i, i ^ k) for i in range(n)])  11 us
    pallas_call x1, Pallas kernels, attention(): pl.pallas_call(functools.partial(attention_kernel, heads, join), out_shap...  3.64 us
    pallas_call x1, Pallas kernels, fetch(): pl.pallas_call(fetch_kernel, out_shape=vmem(weight.shape, weight.dtype),...  2.2 us
    pallas_call x1, Pallas kernels, project(): pl.pallas_call(functools.partial(project_kernel, groups, dps, halves), ou...  0.73 us
  transfers between devices with their start and end apart: 13, of which 9 were waited for; matrix products, arithmetic and copies ran while one was open for 0% of the time, Pallas kernels for 6%

commit v1 on v0

v1 whole, which is shorter than its diff:
```python
import functools
import math

import jax
import jax.numpy as jnp
from jax import lax
from jax.experimental import pallas as pl
from jax.experimental.pallas import tpu as pltpu
from jax.sharding import PartitionSpec as P


F32, BF16 = jnp.float32, jnp.bfloat16
LANES, SUBLANES = 128, 8
MASKED = -1e30
FETCH_FLOPS = 1 << 27


def vmem(shape, dtype):
    return pltpu.VMEM(shape, dtype)


def whole(n):
    return [pl.BlockSpec(memory_space=pltpu.VMEM)] * n


def held(*arrays):
    return [pltpu.with_memory_space_constraint(x, pltpu.VMEM) for x in arrays]


def in_hbm(*arrays):
    return [pltpu.with_memory_space_constraint(x, pltpu.HBM) for x in arrays]


def fetch_kernel(_, w_hbm, w_ref, sem):
    copy = pltpu.make_async_copy(w_hbm, w_ref, sem)
    copy.start()
    copy.wait()


def fetch(after, weight):
    return pl.pallas_call(
        fetch_kernel,
        out_shape=vmem(weight.shape, weight.dtype),
        in_specs=[pl.BlockSpec(memory_space=pltpu.VMEM), pl.BlockSpec(memory_space=pltpu.HBM)],
        out_specs=pl.BlockSpec(memory_space=pltpu.VMEM),
        scratch_shapes=[pltpu.SemaphoreType.DMA],
        cost_estimate=pl.CostEstimate(flops=FETCH_FLOPS, bytes_accessed=weight.size * 2, transcendentals=0),
        compiler_params=pltpu.CompilerParams(vmem_limit_bytes=1 << 20),
        name="fetch",
    )(*held(after), *in_hbm(weight))


def split3(x):
    hi = x.astype(BF16)
    rest = x - hi.astype(F32)
    mid = rest.astype(BF16)
    return hi, mid, (rest - mid.astype(F32)).astype(BF16)


def pack_stats(m, l, heads):
    lane = lax.broadcasted_iota(jnp.int32, m.shape, 1)
    out = jnp.zeros(m.shape, F32)
    for i, part in enumerate(split3(m) + split3(l)):
        term = jnp.where(lane < heads, part.astype(F32), 0.0)
        out = out + (pltpu.roll(term, i * heads, 1) if i else term)
    return out.astype(BF16)


def unpack_stats(packed, heads):
    x = packed.astype(F32)
    lane = lax.broadcasted_iota(jnp.int32, x.shape, 1)

    def term(i):
        return pltpu.roll(x, LANES - i * heads, 1) if i else x

    m = (term(0) + term(1)) + term(2)
    l = (term(3) + term(4)) + term(5)
    return jnp.where(lane < heads, m, 0.0), jnp.where(lane < heads, l, 0.0)


def attend(heads, join, q_ref, k_ref, v_ref, gap_ref, f_scr, o_ref, s_ref):
    rows, steps, _ = q_ref.shape
    span, _, dim = k_ref.shape[1:]
    parts, m_rows = heads // join, join * steps
    scale = 1.0 / math.sqrt(dim)
    lane = lax.broadcasted_iota(jnp.int32, (m_rows, LANES), 1)
    srow = lax.broadcasted_iota(jnp.int32, (m_rows, LANES), 0)
    allowed = [gap_ref[r] < 1 for r in range(rows)]
    units = [(part, r) for part in range(parts) for r in range(rows)]
    for u, (part, r) in enumerate(units):
        for j in range(join):
            f_scr[u, pl.ds(j * steps, steps), :] = q_ref[r, :, pl.ds((part * join + j) * dim, dim)].astype(F32)
    s = [
        lax.dot_general(
            f_scr[u].astype(BF16), k_ref[r, part * span // parts],
            (((1,), (1,)), ((), ())), preferred_element_type=F32,
        )
        for u, (part, r) in enumerate(units)
    ]
    s = [jnp.where(allowed[r], x * scale, MASKED) for x, (_, r) in zip(s, units)]
    m = [jnp.max(x, axis=1, keepdims=True) for x in s]
    p = [jnp.where(allowed[r], jnp.exp(x - y), 0.0) for x, y, (_, r) in zip(s, m, units)]
    l = [jnp.sum(x, axis=1, keepdims=True) for x in p]
    o = [
        jnp.dot(x.astype(BF16), v_ref[r, part * span // parts], preferred_element_type=F32)
        for x, (part, r) in zip(p, units)
    ]
    for x, (part, r) in zip(o, units):
        for j in range(join):
            o_ref[pl.ds(r * steps, steps), pl.ds((part * join + j) * dim, dim)] = x[j * steps : (j + 1) * steps]
    for i, stat in enumerate((m, l)):
        for r in range(rows):
            total = 0.0
            for x, (part, at) in zip(stat, units):
                if at == r:
                    x = jnp.where(lane == part * join + srow // steps, x, 0.0)
                    for b in range(0, m_rows, SUBLANES):
                        total = total + x[b : b + SUBLANES]
            shift = steps
            while shift < SUBLANES:
                total = total + pltpu.roll(total, shift, 0)
                shift *= 2
            s_ref[i, pl.ds(r * steps, steps), :] = total[:steps]


def attend_packed(heads, join, q_ref, k_ref, v_ref, gap_ref, f_scr, o_scr, s_scr, send_ref):
    attend(heads, join, q_ref, k_ref, v_ref, gap_ref, f_scr, o_scr, s_scr)
    width = o_scr.shape[1]
    send_ref[:, pl.ds(0, width)] = o_scr[...].astype(BF16)
    send_ref[:, pl.ds(width, LANES)] = pack_stats(s_scr[0], s_scr[1], heads)


def first_kernel(heads, join, chunks, order, len_hbm, q_hbm, k_hbm, v_hbm, send_ref, q_ref, k_ref, v_ref, gap_ref, len_scr, f_scr, o_scr, s_scr, sems):
    rows = q_hbm.shape[0]
    kv_heads, cache, dim = k_hbm.shape[1:]
    q_heads = q_hbm.shape[2] // dim
    tensor, width, span = q_heads // heads, heads * dim, k_ref.shape[2]
    me = lax.axis_index("tensor")
    copies = []
    for chunk in range(tensor):
        owner = me ^ chunk
        kv = owner * heads // (q_heads // kv_heads)
        copies.append([
            pltpu.make_async_copy(q_hbm.at[:, :, pl.ds(pl.multiple_of(owner * width, width), width)], q_ref.at[chunk], sems.at[0, chunk]),
            pltpu.make_async_copy(k_hbm.at[:, pl.ds(kv, span)], k_ref.at[chunk], sems.at[1, chunk]),
            pltpu.make_async_copy(v_hbm.at[:, pl.ds(kv, span)], v_ref.at[chunk], sems.at[2, chunk]),
        ])
    limits = pltpu.make_async_copy(len_hbm, len_scr, sems.at[3, 0])
    limits.start()
    for chunk in order:
        for copy in copies[chunk]:
            copy.start()
    limits.wait()
    shape = gap_ref.shape[1:]
    row = lax.broadcasted_iota(jnp.int32, shape, 0)
    steps = q_hbm.shape[1]
    position = me * cache + lax.broadcasted_iota(jnp.int32, shape, 1) - row % steps
    for r in range(rows):
        gap_ref[r] = position - len_scr[r]
    for i, chunk in enumerate(chunks):
        for copy in copies[chunk]:
            copy.wait()
        attend_packed(heads, join, q_ref.at[chunk], k_ref.at[chunk], v_ref.at[chunk], gap_ref, f_scr.at[i], o_scr.at[i], s_scr.at[i], send_ref.at[i])
    for chunk in order:
        if chunk not in chunks:
            for copy in copies[chunk]:
                copy.wait()


def send_kernel(heads, join, chunk, q_ref, k_ref, v_ref, gap_ref, send_ref, f_scr, o_scr, s_scr):
    attend_packed(heads, join, q_ref.at[chunk], k_ref.at[chunk], v_ref.at[chunk], gap_ref, f_scr, o_scr, s_scr, send_ref)


def keep_kernel(heads, join, chunks, q_ref, k_ref, v_ref, gap_ref, acc_ref, stat_ref, f_scr):
    for i, c in enumerate(chunks):
        attend(heads, join, q_ref.at[c], k_ref.at[c], v_ref.at[c], gap_ref, f_scr.at[i], acc_ref.at[i], stat_ref.at[i])


class Attention:
    def __init__(self, queries, keys, tensor):
        self.rows, self.steps, model = queries.shape
        kv_heads, self.cache, self.dim = keys.shape[1:]
        q_heads = model // self.dim
        per_kv = q_heads // kv_heads
        self.tensor, self.heads = tensor, q_heads // tensor
        self.join, self.span = min(self.heads, per_kv), max(1, self.heads // per_kv)
        self.width, self.tokens = self.heads * self.dim, self.rows * self.steps
        self.m_rows = self.join * self.steps

    def scratch(self, n):
        lead = (n,) if n else ()
        return [
            pltpu.VMEM((*lead, self.rows * self.heads // self.join, self.m_rows, self.dim), F32),
            pltpu.VMEM((*lead, self.tokens, self.width), F32),
            pltpu.VMEM((*lead, 2, self.tokens, LANES), F32),
        ]

    def options(self, n):
        work = 4 * n * self.tokens * self.width * self.cache
        return dict(
            cost_estimate=pl.CostEstimate(flops=4 * work, bytes_accessed=0, transcendentals=0),
            compiler_params=pltpu.CompilerParams(vmem_limit_bytes=8 << 20),
        )

    def first(self, chunks, order, lengths, queries, keys, values):
        cached = (self.tensor, self.rows, self.span, self.cache, self.dim)
        return pl.pallas_call(
            functools.partial(first_kernel, self.heads, self.join, chunks, order),
            out_shape=(
                vmem((len(chunks), self.tokens, self.width + LANES), BF16),
                vmem((self.tensor, self.rows, self.steps, self.width), BF16),
                vmem(cached, BF16),
                vmem(cached, BF16),
                vmem((self.rows, self.m_rows, self.cache), jnp.int32),
            ),
            in_specs=[pl.BlockSpec(memory_space=pltpu.HBM)] * 4,
            out_specs=whole(5),
            scratch_shapes=[pltpu.SMEM((self.rows,), jnp.int32)] + self.scratch(len(chunks)) + [pltpu.SemaphoreType.DMA((4, self.tensor))],
            name="attend_first",
            **self.options(len(chunks)),
        )(*in_hbm(lengths, queries, keys, values))

    def send(self, chunk, *loaded):
        return pl.pallas_call(
            functools.partial(send_kernel, self.heads, self.join, chunk),
            out_shape=vmem((self.tokens, self.width + LANES), BF16),
            in_specs=whole(4),
            out_specs=pl.BlockSpec(memory_space=pltpu.VMEM),
            scratch_shapes=self.scratch(0),
            name="attend_send",
            **self.options(1),
        )(*held(*loaded))

    def keep(self, chunks, *loaded):
        n = len(chunks)
        return pl.pallas_call(
            functools.partial(keep_kernel, self.heads, self.join, chunks),
            out_shape=(vmem((n, self.tokens, self.width), F32), vmem((n, 2, self.tokens, LANES), F32)),
            in_specs=whole(4),
            out_specs=whole(2),
            scratch_shapes=self.scratch(n)[:1],
            name="attend_keep",
            **self.options(n),
        )(*held(*loaded))


def merged(acc, m, l, received, heads):
    width = acc.shape[1]
    dim = width // heads
    m2, l2 = unpack_stats(received[:, width:], heads)
    top = jnp.maximum(m, m2)
    e1, e2 = jnp.exp(m - top), jnp.exp(m2 - top)
    columns = [
        e1[:, i : i + 1] * acc[:, i * dim : (i + 1) * dim]
        + e2[:, i : i + 1] * received[:, i * dim : (i + 1) * dim].astype(F32)
        for i in range(heads)
    ]
    return columns, top, e1 * l + e2 * l2


def core_merge_kernel(heads, acc_ref, stat_ref, recv_ref, send_ref):
    width = acc_ref.shape[2]
    dim = width // heads
    for k in range(acc_ref.shape[0]):
        columns, m, l = merged(acc_ref[k], stat_ref[k, 0], stat_ref[k, 1], recv_ref[k], heads)
        for i, c in enumerate(columns):
            send_ref[k, :, pl.ds(i * dim, dim)] = c.astype(BF16)
        send_ref[k, :, pl.ds(width, LANES)] = pack_stats(m, l, heads)


def core_merge(acc, stat, received, heads):
    return pl.pallas_call(
        functools.partial(core_merge_kernel, heads),
        out_shape=vmem(received.shape, BF16),
        in_specs=whole(3),
        out_specs=pl.BlockSpec(memory_space=pltpu.VMEM),
        compiler_params=pltpu.CompilerParams(vmem_limit_bytes=4 << 20),
        name="core_merge",
    )(*held(acc, stat, received))


def near_merge_kernel(heads, acc_ref, stat_ref, recv_ref, own_ref, own_stat_ref):
    dim = acc_ref.shape[2] // heads
    columns, m, l = merged(acc_ref[0], stat_ref[0, 0], stat_ref[0, 1], recv_ref[...], heads)
    for i, c in enumerate(columns):
        own_ref[:, pl.ds(i * dim, dim)] = c
    own_stat_ref[0] = m
    own_stat_ref[1] = l


def near_merge(acc, stat, received, heads):
    return pl.pallas_call(
        functools.partial(near_merge_kernel, heads),
        out_shape=(vmem(acc.shape[1:], F32), vmem(stat.shape[1:], F32)),
        in_specs=whole(3),
        out_specs=whole(2),
        cost_estimate=pl.CostEstimate(flops=1 << 22, bytes_accessed=0, transcendentals=0),
        compiler_params=pltpu.CompilerParams(vmem_limit_bytes=4 << 20),
        name="near_merge",
    )(*held(acc, stat, received))


def final_merge_kernel(heads, n, own_ref, stat_ref, *refs):
    recv, out_ref = refs[:n], refs[n]
    width = own_ref.shape[1]
    dim = width // heads
    stats = [(stat_ref[0], stat_ref[1])] + [unpack_stats(r[:, pl.ds(width, LANES)], heads) for r in recv]
    top = functools.reduce(jnp.maximum, [m for m, _ in stats])
    weights = [jnp.exp(m - top) for m, _ in stats]
    inverse = 1.0 / sum(w * l for w, (_, l) in zip(weights, stats))
    weights = [w * inverse for w in weights]
    for i in range(heads):
        columns = pl.ds(i * dim, dim)
        total = weights[0][:, i : i + 1] * own_ref[:, columns]
        for w, r in zip(weights[1:], recv):
            total = total + w[:, i : i + 1] * r[:, columns].astype(F32)
        out_ref[:, columns] = total.astype(BF16)


def final_merge(own, stat, received, heads):
    return pl.pallas_call(
        functools.partial(final_merge_kernel, heads, len(received)),
        out_shape=vmem(own.shape, BF16),
        in_specs=whole(2 + len(received)),
        out_specs=pl.BlockSpec(memory_space=pltpu.VMEM),
        compiler_params=pltpu.CompilerParams(vmem_limit_bytes=8 << 20),
        name="final_merge",
    )(*held(own, stat, *received))


def project_kernel(n, *refs):
    blocks, w_ref = refs[:n], refs[n]
    send_ref, keep_ref, lhs = refs[n + 1 :]
    tokens = blocks[0].shape[0]
    twist = lax.axis_index("dp") ^ lax.axis_index("tensor")
    for kd in range(n):
        at = twist ^ kd
        lhs[pl.ds(pl.multiple_of(at * tokens, tokens), tokens), :] = blocks[kd][...]
    out = jnp.dot(lhs[...], w_ref[...], preferred_element_type=F32)
    for kt in range(n):
        piece = out[kt * tokens : (kt + 1) * tokens]
        if kt % 2:
            send_ref[kt // 2] = piece.astype(BF16)
        else:
            keep_ref[kt // 2] = piece


def project(blocks, weight):
    n, (tokens, width), columns = len(blocks), blocks[0].shape, weight.shape[1]
    shape = (n // 2, tokens, columns)
    return pl.pallas_call(
        functools.partial(project_kernel, n),
        out_shape=(vmem(shape, BF16), vmem(shape, F32)),
        in_specs=whole(n + 1),
        out_specs=whole(2),
        scratch_shapes=[pltpu.VMEM((n * tokens, width), BF16)],
        cost_estimate=pl.CostEstimate(flops=2 * n * tokens * width * columns, bytes_accessed=0, transcendentals=0),
        compiler_params=pltpu.CompilerParams(vmem_limit_bytes=8 << 20),
        name="project",
    )(*held(*blocks, weight))


def swap(x, axes, n, k):
    return lax.ppermute(x, axes, [(i, i ^ k) for i in range(n)])


def on_device(queries, keys, values, cached_length, out_weight):
    _, _, model = queries.shape
    q_heads = model // keys.shape[3]
    tensor, groups, dps = lax.axis_size("tensor"), lax.axis_size("group"), lax.axis_size("dp")
    halves, heads = tensor // 2, q_heads // tensor

    plan = Attention(queries, keys, tensor)
    far = list(range(3, tensor, 2))
    order = far + [c - 1 for c in far] + [1, 0]
    send, *loaded = plan.first(far, order, cached_length, queries, keys, values)
    received = swap(send, "tensor", tensor, 1)
    acc, stat = plan.keep([c - 1 for c in far], *loaded)
    send = core_merge(acc, stat, received, heads)
    arrived = []
    for k in range(1, halves):
        arrived.append(swap(send[k - 1], "tensor", tensor, 2 * k))
    near = plan.send(1, *loaded)
    near = swap(near, "tensor", tensor, 1)
    acc, stat = plan.keep([0], *loaded)
    own, stat = near_merge(acc, stat, near, heads)
    attended = final_merge(own, stat, arrived, heads)

    weight = fetch(attended, out_weight)
    line = [attended]
    for k in range(1, dps):
        line.append(swap(attended, "dp", dps, k))
    plane, n = ("group", "tensor"), groups * tensor
    sums = []
    for kg in range(groups):
        blocks = line
        if kg:
            blocks = []
            for b in line:
                blocks.append(swap(b, "group", groups, kg))
        send, keep = project(blocks, weight)
        both = keep + swap(send, "tensor", tensor, 1).astype(F32)
        total = 0.0 if kg else both[0]
        for kx in range(halves):
            if kg or kx:
                total = total + swap(both[kx].astype(BF16), plane, n, kg * tensor + 2 * kx).astype(F32)
        sums.append(total)
    me = lax.axis_index("group")
    placed = []
    for g in range(groups):
        kept = sums[0]
        for kg in range(1, groups):
            kept = jnp.where(me ^ kg == g, sums[kg], kept)
        placed.append(kept)
    return jnp.stack(placed, axis=1).astype(BF16)


def solution(mesh):
    in_specs = (
        P(("group", "dp"), None, None),
        P(("group", "dp"), None, "tensor", None),
        P(("group", "dp"), None, "tensor", None),
        P(("group", "dp")),
        P("tensor", ("group", "dp")),
    )
    out_specs = P(("group", "tensor"), None, "dp")
    return jax.shard_map(
        on_device, mesh=mesh, in_specs=in_specs, out_specs=out_specs, check_vma=False
    )
```

time: 36.3 us -> 33.8 us (0.931)
  waiting for transfers between devices: 11 us -> 6.87 us
  starting transfers between devices: 16.9 us -> 18.1 us
  Pallas kernels: 7.28 us -> 7.78 us
    ppermute x13 -> x15, waiting for transfers between devices: 11 us -> 6.87 us  [swap(): return lax.ppermute(x, axes, [(i, i ^ k) for i in range(n)])]
    ppermute x13 -> x15, starting transfers between devices: 16.9 us -> 18.1 us  [swap(): return lax.ppermute(x, axes, [(i, i ^ k) for i in range(n)])]
    pallas_call x3 -> x8, Pallas kernels: 4.79 us -> 5.33 us  [the longest x1 1.74 us: first(): pl.pallas_call(functools.partial(first_kernel, self.heads, self.join, chu...]
  transfers between devices with their start and end apart: 13 -> 15, of which waited for: 9 -> 6; matrix products, arithmetic and copies ran while one was open for 0% -> 0% of each run, Pallas kernels for 6% -> 17%
where the time goes in v1:
time: 33.8 us; the launch traced here: 33.7 us
  starting transfers between devices  18.1 us (54%)
  Pallas kernels  7.78 us (23%)
  waiting for transfers between devices  6.87 us (20%)
  local copies, waits for them, and re-layouts  0.71 us (2%)
    ppermute x15, starting transfers between devices, swap(): return lax.ppermute(x, axes, [(i, i ^ k) for i in range(n)])  18.1 us
    ppermute x15, waiting for transfers between devices, swap(): return lax.ppermute(x, axes, [(i, i ^ k) for i in range(n)])  6.87 us
    pallas_call x1, Pallas kernels, fetch(): pl.pallas_call(fetch_kernel, out_shape=vmem(weight.shape, weight.dtype),...  2.2 us
    pallas_call x1, Pallas kernels, first(): pl.pallas_call(functools.partial(first_kernel, self.heads, self.join, chu...  1.74 us
    pallas_call x2, Pallas kernels, project(): pl.pallas_call(functools.partial(project_kernel, n), out_shape=(vmem(shap...  1.69 us
    pallas_call x2, Pallas kernels, keep(): pl.pallas_call(functools.partial(keep_kernel, self.heads, self.join, chun...  0.91 us
    another operation x1, local copies, waits for them, and re-layouts, on_device(): return jnp.stack(placed, axis=1).astype(BF16)  0.7 us
  transfers between devices with their start and end apart: 15, of which 6 were waited for; matrix products, arithmetic and copies ran while one was open for 0% of the time, Pallas kernels for 17%

profile of v1, /device:TPU:0, one launch (start us, length us, event | category | flops | bytes accessed | tf_op | source)
XLA Modules:
  0.0 33.7 jit_solution(12600830021183141537)
XLA Ops:
  0.0 1.7 %attend_first.1 = (bf16[1,16,2176]{2,1,0:T(8,128)(2,1)S(1)}, bf16[4,4,4,2048]{3,2,1,0:T(4,128)(2,1)S(1)}, bf16[4,4,2,128,128]{4,3,2,1,0:T(8,128)(2,1)S(1)}, bf16...) custom-call(s32[4]{0:T(128)} %len_hbm.1, bf16[4,4,8192]{2,1,0:T(4,128)(2,1)} %q_hbm.1, ...), custom_call_target="tpu_custom_call" | custom-call | flops 67108864 | tf_op jit(solution)/shard_map/attend_first/pallas_call | solution.py:207
  1.7 0.6 %collective-permute-start.1 = (bf16[1,16,2176]{2,1,0:T(8,128)(2,1)S(1)}, bf16[1,16,2176]{2,1,0:T(8,128)(2,1)S(1)}, u32[]{:S(2)}, u32[]{:S(2)}) collective-permute-start(bf16[1,16,2176]{2,1,0:T(8,128)(2,1)S(1)} %get-tuple-element.30), channel_id=1, source_target_pairs={{0,1},{1,0},{2,3},{3,2},{4,5},{5,4},{6,7},{7,6},{8,9},{9,8},{10,11... | collective-permute-start | bytes 208904 | tf_op jit(solution)/shard_map/ppermute | solution.py:364
  2.3 0.5 %attend_send.1 = bf16[16,2176]{1,0:T(8,128)(2,1)S(1)} custom-call(bf16[4,4,4,2048]{3,2,1,0:T(4,128)(2,1)S(1)} %get-tuple-element.20.q_ref, bf16[4,4,2,128,128]{4,3,2,1,0:T(8,128)(2,1)S(1)} %get-tuple-element.21.k_ref, bf16[4,4,2,128,128]{4,3,2,1,0:T(8,128)(2,1)S(1)} %get-tuple-element.22.v_ref, s32[4,32,128]{2,1,0:T(8,128)S(1)} %get-tuple-element.23.gap_ref), custom_call_target="tpu_custom_call" | custom-call | flops 67108864 | tf_op jit(solution)/shard_map/attend_send/pallas_call | solution.py:224
  2.8 0.0 collective-permute-start
  2.9 0.5 %attend_keep.3 = (f32[1,16,2048]{2,1,0:T(8,128)S(1)}, f32[1,2,16,128]{3,2,1,0:T(8,128)S(1)}) custom-call(bf16[4,4,4,2048]{3,2,1,0:T(4,128)(2,1)S(1)} %get-tuple-element.20.q_ref, bf16[4,4,2,128,128]{4,3,2,1,0:T(8,128)(2,1)S(1)} %get-tuple-element.21.k_ref, bf16[4,4,2,128,128]{4,3,2,1,0:T(8,128)(2,1)S(1)} %get-tuple-element.22.v_ref, ...), custom_call_target="tpu_custom_call" | custom-call | flops 67108864 | tf_op jit(solution)/shard_map/attend_keep/pallas_call | solution.py:236
  3.3 0.0 collective-permute-done.1.recv_ref
  3.3 0.2 core_merge.1
  3.6 3.0 %collective-permute-start.2 = (bf16[16,2176]{1,0:T(8,128)(2,1)S(1)}, bf16[16,2176]{1,0:T(8,128)(2,1)S(1)}, u32[]{:S(2)}, u32[]{:S(2)}) collective-permute-start(bf16[16,2176]{1,0:T(8,128)(2,1)S(1)} %bitcast.23), channel_id=1, source_target_pairs={{0,2},{1,3},{2,0},{3,1},{4,6},{5,7},{6,4},{7,5},{8,10},{9,11},{10,... | collective-permute-start | bytes 208904 | tf_op jit(solution)/shard_map/ppermute | solution.py:364
  6.6 0.5 %attend_keep.2 = (f32[1,16,2048]{2,1,0:T(8,128)S(1)}, f32[1,2,16,128]{3,2,1,0:T(8,128)S(1)}) custom-call(bf16[4,4,4,2048]{3,2,1,0:T(4,128)(2,1)S(1)} %get-tuple-element.20.q_ref, bf16[4,4,2,128,128]{4,3,2,1,0:T(8,128)(2,1)S(1)} %get-tuple-element.21.k_ref, bf16[4,4,2,128,128]{4,3,2,1,0:T(8,128)(2,1)S(1)} %get-tuple-element.22.v_ref, ...), custom_call_target="tpu_custom_call" | custom-call | flops 67108864 | tf_op jit(solution)/shard_map/attend_keep/pallas_call | solution.py:236
  7.1 0.0 collective-permute-done.recv_ref
  7.1 0.2 near_merge.1
  7.3 1.7 %collective-permute-done.2.refs_0_ = bf16[16,2176]{1,0:T(8,128)(2,1)S(1)} collective-permute-done((bf16[16,2176]{1,0:T(8,128)(2,1)S(1)}, bf16[16,2176]{1,0:T(8,128)(2,1)S(1)}, u32[]{:S(2)}, u32[]{:S(2)}) %collective-permute-start.2) | collective-permute-done | bytes 69664 | tf_op jit(solution)/shard_map/ppermute | solution.py:364
  9.0 0.2 final_merge.1._.refs_0_
  9.2 2.1 %collective-permute-start.4 = (bf16[16,2048]{1,0:T(8,128)(2,1)S(1)}, bf16[16,2048]{1,0:T(8,128)(2,1)S(1)}, u32[]{:S(2)}, u32[]{:S(2)}) collective-permute-start(bf16[16,2048]{1,0:T(8,128)(2,1)S(1)} %final_merge.1._.refs_0_), channel_id=1, source_target_pairs={{0,4},{4,0},{8,12},{12,8},{1,5},{5,1},{9,13},{13,9},{2,6},{6,2},{1... | collective-permute-start | bytes 196616 | tf_op jit(solution)/shard_map/ppermute | solution.py:364
  11.3 2.6 %collective-permute-start.6 = (bf16[16,2048]{1,0:T(8,128)(2,1)S(1)}, bf16[16,2048]{1,0:T(8,128)(2,1)S(1)}, u32[]{:S(2)}, u32[]{:S(2)}) collective-permute-start(bf16[16,2048]{1,0:T(8,128)(2,1)S(1)} %final_merge.1._.refs_0_), channel_id=1, source_target_pairs={{0,8},{4,12},{8,0},{12,4},{1,9},{5,13},{9,1},{13,5},{2,10},{6,14},... | collective-permute-start | bytes 196616 | tf_op jit(solution)/shard_map/ppermute | solution.py:364
  13.9 0.0 collective-permute-start.8
  13.9 1.7 %collective-permute-start.3 = (bf16[16,2048]{1,0:T(8,128)(2,1)S(1)}, bf16[16,2048]{1,0:T(8,128)(2,1)S(1)}, u32[]{:S(2)}, u32[]{:S(2)}) collective-permute-start(bf16[16,2048]{1,0:T(8,128)(2,1)S(1)} %final_merge.1._.refs_0_), channel_id=1, source_target_pairs={{0,16},{16,0},{1,17},{17,1},{2,18},{18,2},{3,19},{19,3},{4,20},{20... | collective-permute-start | bytes 196616 | tf_op jit(solution)/shard_map/ppermute | solution.py:364
  15.7 0.0 collective-permute-done.4.refs_1_
  15.7 0.5 %collective-permute-start.5 = (bf16[16,2048]{1,0:T(8,128)(2,1)S(1)}, bf16[16,2048]{1,0:T(8,128)(2,1)S(1)}, u32[]{:S(2)}, u32[]{:S(2)}) collective-permute-start(bf16[16,2048]{1,0:T(8,128)(2,1)S(1)} %collective-permute-done.4.refs_1_), channel_id=1, source_target_pairs={{0,16},{16,0},{1,17},{17,1},{2,18},{18,2},{3,19},{19,3},{4,20},{20... | collective-permute-start | bytes 196616 | tf_op jit(solution)/shard_map/ppermute | solution.py:364
  16.2 1.7 %collective-permute-done.6.refs_2_ = bf16[16,2048]{1,0:T(8,128)(2,1)S(1)} collective-permute-done((bf16[16,2048]{1,0:T(8,128)(2,1)S(1)}, bf16[16,2048]{1,0:T(8,128)(2,1)S(1)}, u32[]{:S(2)}, u32[]{:S(2)}) %collective-permute-start.6) | collective-permute-done | bytes 65568 | tf_op jit(solution)/shard_map/ppermute | solution.py:364
  17.9 1.5 %collective-permute-start.7 = (bf16[16,2048]{1,0:T(8,128)(2,1)S(1)}, bf16[16,2048]{1,0:T(8,128)(2,1)S(1)}, u32[]{:S(2)}, u32[]{:S(2)}) collective-permute-start(bf16[16,2048]{1,0:T(8,128)(2,1)S(1)} %collective-permute-done.6.refs_2_), channel_id=1, source_target_pairs={{0,16},{16,0},{1,17},{17,1},{2,18},{18,2},{3,19},{19,3},{4,20},{20... | collective-permute-start | bytes 196616 | tf_op jit(solution)/shard_map/ppermute | solution.py:364
  19.4 0.6 %collective-permute-done.8.refs_3_ = bf16[16,2048]{1,0:T(8,128)(2,1)S(1)} collective-permute-done((bf16[16,2048]{1,0:T(8,128)(2,1)S(1)}, bf16[16,2048]{1,0:T(8,128)(2,1)S(1)}, u32[]{:S(2)}, u32[]{:S(2)}) %collective-permute-start.8) | collective-permute-done | bytes 65568 | tf_op jit(solution)/shard_map/ppermute | solution.py:364
  20.0 1.5 %collective-permute-start.9 = (bf16[16,2048]{1,0:T(8,128)(2,1)S(1)}, bf16[16,2048]{1,0:T(8,128)(2,1)S(1)}, u32[]{:S(2)}, u32[]{:S(2)}) collective-permute-start(bf16[16,2048]{1,0:T(8,128)(2,1)S(1)} %collective-permute-done.8.refs_3_), channel_id=1, source_target_pairs={{0,16},{16,0},{1,17},{17,1},{2,18},{18,2},{3,19},{19,3},{4,20},{20... | collective-permute-start | bytes 196616 | tf_op jit(solution)/shard_map/ppermute | solution.py:364
  21.5 2.2 %fetch.1.refs_4_ = bf16[2048,1024]{1,0:T(8,128)(2,1)S(1)} custom-call(bf16[16,2048]{1,0:T(8,128)(2,1)S(1)} %final_merge.1._.refs_0_, bf16[2048,1024]{1,0:T(8,128)(2,1)} %w_hbm.1), custom_call_target="tpu_custom_call" | custom-call | flops 134217728 | bytes 4194304 | tf_op jit(solution)/shard_map/fetch/pallas_call | solution.py:41
  23.7 0.8 %project.3 = (bf16[2,16,1024]{2,1,0:T(8,128)(2,1)S(1)}, f32[2,16,1024]{2,1,0:T(8,128)S(1)}) custom-call(bf16[16,2048]{1,0:T(8,128)(2,1)S(1)} %final_merge.1._.refs_0_, bf16[16,2048]{1,0:T(8,128)(2,1)S(1)} %collective-permute-done.4.refs_1_, bf16[16,2048]{1,0:T(8,128)(2,1)S(1)} %collective-permute-done.6.refs_2_, ...), custom_call_target="tpu_custom_call" | custom-call | flops 268435456 | tf_op jit(solution)/shard_map/project/pallas_call | solution.py:351
  24.6 0.1 collective-permute-start.13
  24.6 0.0 collective-permute-done.3.refs_0_
  24.6 0.0 collective-permute-done.5.refs_1_
  24.7 0.0 collective-permute-done.7.refs_2_
  24.7 0.0 collective-permute-done.9.refs_3_
  24.7 0.8 %project.2 = (bf16[2,16,1024]{2,1,0:T(8,128)(2,1)S(1)}, f32[2,16,1024]{2,1,0:T(8,128)S(1)}) custom-call(bf16[16,2048]{1,0:T(8,128)(2,1)S(1)} %collective-permute-done.3.refs_0_, bf16[16,2048]{1,0:T(8,128)(2,1)S(1)} %collective-permute-done.5.refs_1_, bf16[16,2048]{1,0:T(8,128)(2,1)S(1)} %collective-permute-done.7.refs_2_, ...), custom_call_target="tpu_custom_call" | custom-call | flops 268435456 | tf_op jit(solution)/shard_map/project/pallas_call | solution.py:351
  25.5 0.5 %collective-permute-start.10 = (bf16[2,16,1024]{2,1,0:T(8,128)(2,1)S(1)}, bf16[2,16,1024]{2,1,0:T(8,128)(2,1)S(1)}, u32[]{:S(2)}, u32[]{:S(2)}) collective-permute-start(bf16[2,16,1024]{2,1,0:T(8,128)(2,1)S(1)} %get-tuple-element.32), channel_id=1, source_target_pairs={{0,1},{1,0},{2,3},{3,2},{4,5},{5,4},{6,7},{7,6},{8,9},{9,8},{10,11... | collective-permute-start | bytes 196616 | tf_op jit(solution)/shard_map/ppermute | solution.py:364
  26.1 0.0 collective-permute-done.13
  26.1 1.6 %collective-permute-start.14 = (bf16[16,1024]{1,0:T(8,128)(2,1)S(1)}, bf16[16,1024]{1,0:T(8,128)(2,1)S(1)}, u32[]{:S(2)}, u32[]{:S(2)}) collective-permute-start(bf16[16,1024]{1,0:T(8,128)(2,1)S(1)} %fusion.3), channel_id=1, source_target_pairs={{0,2},{1,3},{2,0},{3,1},{16,18},{17,19},{18,16},{19,17},{4,6},{5,7... | collective-permute-start | bytes 98312 | tf_op jit(solution)/shard_map/ppermute | solution.py:364
  27.7 0.0 collective-permute-done.10
  27.7 1.3 %collective-permute-start.12 = (bf16[16,1024]{1,0:T(8,128)(2,1)S(1)}, bf16[16,1024]{1,0:T(8,128)(2,1)S(1)}, u32[]{:S(2)}, u32[]{:S(2)}) collective-permute-start(bf16[16,1024]{1,0:T(8,128)(2,1)S(1)} %get-tuple-element.38), channel_id=1, source_target_pairs={{0,18},{1,19},{2,16},{3,17},{16,2},{17,3},{18,0},{19,1},{4,22},{5,... | collective-permute-start | bytes 98312 | tf_op jit(solution)/shard_map/ppermute | solution.py:364
  29.0 1.1 %collective-permute-start.11 = (bf16[16,1024]{1,0:T(8,128)(2,1)S(1)}, bf16[16,1024]{1,0:T(8,128)(2,1)S(1)}, u32[]{:S(2)}, u32[]{:S(2)}) collective-permute-start(bf16[16,1024]{1,0:T(8,128)(2,1)S(1)} %get-tuple-element.37), channel_id=1, source_target_pairs={{0,16},{1,17},{2,18},{3,19},{16,0},{17,1},{18,2},{19,3},{4,20},{5,... | collective-permute-start | bytes 98312 | tf_op jit(solution)/shard_map/ppermute | solution.py:364
  30.0 0.1 collective-permute-done.14
  30.1 2.5 %collective-permute-done.12 = bf16[16,1024]{1,0:T(8,128)(2,1)S(1)} collective-permute-done((bf16[16,1024]{1,0:T(8,128)(2,1)S(1)}, bf16[16,1024]{1,0:T(8,128)(2,1)S(1)}, u32[]{:S(2)}, u32[]{:S(2)}) %collective-permute-start.12) | collective-permute-done | bytes 32800 | tf_op jit(solution)/shard_map/ppermute | solution.py:364
  32.6 0.4 %collective-permute-done.11 = bf16[16,1024]{1,0:T(8,128)(2,1)S(1)} collective-permute-done((bf16[16,1024]{1,0:T(8,128)(2,1)S(1)}, bf16[16,1024]{1,0:T(8,128)(2,1)S(1)}, u32[]{:S(2)}, u32[]{:S(2)}) %collective-permute-start.11) | collective-permute-done | bytes 32800 | tf_op jit(solution)/shard_map/ppermute | solution.py:364
  33.0 0.7 %copy.6 = bf16[16,2,1024]{2,1,0:T(2,128)(2,1)} copy(bf16[16,2,1024]{2,0,1:T(8,128)(2,1)S(1)} %pad_maximum_fusion) | data formatting | bytes 131072 | tf_op jit(solution)/shard_map/stack | solution.py:415
  (6 shorter events, 0.1 us)
Async XLA Ops:
  1.7 1.6 %collective-permute-start.1 = (bf16[1,16,2176]{2,1,0:T(8,128)(2,1)S(1)}, bf16[1,16,2176]{2,1,0:T(8,128)(2,1)S(1)}, u32[]{:S(2)}, u32[]{:S(2)}) collective-permute-start(bf16[1,16,2176]{2,1,0:T(8,128)(2,1)S(1)} %get-tuple-element.30), channel_id=1, source_target_pairs={{0,1},{1,0},{2,3},{3,2},{4,5},{5,4},{6,7},{7,6},{8,9},{9,8},{10,11... | collective-permute-start | bytes 208904 | tf_op jit(solution)/shard_map/ppermute | solution.py:364
  2.8 4.2 %collective-permute-start = (bf16[16,2176]{1,0:T(8,128)(2,1)S(1)}, bf16[16,2176]{1,0:T(8,128)(2,1)S(1)}, u32[]{:S(2)}, u32[]{:S(2)}) collective-permute-start(bf16[16,2176]{1,0:T(8,128)(2,1)S(1)} %attend_send.1), channel_id=1, source_target_pairs={{0,1},{1,0},{2,3},{3,2},{4,5},{5,4},{6,7},{7,6},{8,9},{9,8},{10,11... | collective-permute-start | bytes 208904 | tf_op jit(solution)/shard_map/ppermute | solution.py:364
  3.6 5.4 %collective-permute-start.2 = (bf16[16,2176]{1,0:T(8,128)(2,1)S(1)}, bf16[16,2176]{1,0:T(8,128)(2,1)S(1)}, u32[]{:S(2)}, u32[]{:S(2)}) collective-permute-start(bf16[16,2176]{1,0:T(8,128)(2,1)S(1)} %bitcast.23), channel_id=1, source_target_pairs={{0,2},{1,3},{2,0},{3,1},{4,6},{5,7},{6,4},{7,5},{8,10},{9,11},{10,... | collective-permute-start | bytes 208904 | tf_op jit(solution)/shard_map/ppermute | solution.py:364
  9.2 6.4 %collective-permute-start.4 = (bf16[16,2048]{1,0:T(8,128)(2,1)S(1)}, bf16[16,2048]{1,0:T(8,128)(2,1)S(1)}, u32[]{:S(2)}, u32[]{:S(2)}) collective-permute-start(bf16[16,2048]{1,0:T(8,128)(2,1)S(1)} %final_merge.1._.refs_0_), channel_id=1, source_target_pairs={{0,4},{4,0},{8,12},{12,8},{1,5},{5,1},{9,13},{13,9},{2,6},{6,2},{1... | collective-permute-start | bytes 196616 | tf_op jit(solution)/shard_map/ppermute | solution.py:364
  11.3 6.6 %collective-permute-start.6 = (bf16[16,2048]{1,0:T(8,128)(2,1)S(1)}, bf16[16,2048]{1,0:T(8,128)(2,1)S(1)}, u32[]{:S(2)}, u32[]{:S(2)}) collective-permute-start(bf16[16,2048]{1,0:T(8,128)(2,1)S(1)} %final_merge.1._.refs_0_), channel_id=1, source_target_pairs={{0,8},{4,12},{8,0},{12,4},{1,9},{5,13},{9,1},{13,5},{2,10},{6,14},... | collective-permute-start | bytes 196616 | tf_op jit(solution)/shard_map/ppermute | solution.py:364
  13.9 6.1 %collective-permute-start.8 = (bf16[16,2048]{1,0:T(8,128)(2,1)S(1)}, bf16[16,2048]{1,0:T(8,128)(2,1)S(1)}, u32[]{:S(2)}, u32[]{:S(2)}) collective-permute-start(bf16[16,2048]{1,0:T(8,128)(2,1)S(1)} %final_merge.1._.refs_0_), channel_id=1, source_target_pairs={{0,12},{4,8},{8,4},{12,0},{1,13},{5,9},{9,5},{13,1},{2,14},{6,10},... | collective-permute-start | bytes 196616 | tf_op jit(solution)/shard_map/ppermute | solution.py:364
  13.9 10.7 %collective-permute-start.3 = (bf16[16,2048]{1,0:T(8,128)(2,1)S(1)}, bf16[16,2048]{1,0:T(8,128)(2,1)S(1)}, u32[]{:S(2)}, u32[]{:S(2)}) collective-permute-start(bf16[16,2048]{1,0:T(8,128)(2,1)S(1)} %final_merge.1._.refs_0_), channel_id=1, source_target_pairs={{0,16},{16,0},{1,17},{17,1},{2,18},{18,2},{3,19},{19,3},{4,20},{20... | collective-permute-start | bytes 196616 | tf_op jit(solution)/shard_map/ppermute | solution.py:364
  15.7 9.0 %collective-permute-start.5 = (bf16[16,2048]{1,0:T(8,128)(2,1)S(1)}, bf16[16,2048]{1,0:T(8,128)(2,1)S(1)}, u32[]{:S(2)}, u32[]{:S(2)}) collective-permute-start(bf16[16,2048]{1,0:T(8,128)(2,1)S(1)} %collective-permute-done.4.refs_1_), channel_id=1, source_target_pairs={{0,16},{16,0},{1,17},{17,1},{2,18},{18,2},{3,19},{19,3},{4,20},{20... | collective-permute-start | bytes 196616 | tf_op jit(solution)/shard_map/ppermute | solution.py:364
  17.9 6.8 %collective-permute-start.7 = (bf16[16,2048]{1,0:T(8,128)(2,1)S(1)}, bf16[16,2048]{1,0:T(8,128)(2,1)S(1)}, u32[]{:S(2)}, u32[]{:S(2)}) collective-permute-start(bf16[16,2048]{1,0:T(8,128)(2,1)S(1)} %collective-permute-done.6.refs_2_), channel_id=1, source_target_pairs={{0,16},{16,0},{1,17},{17,1},{2,18},{18,2},{3,19},{19,3},{4,20},{20... | collective-permute-start | bytes 196616 | tf_op jit(solution)/shard_map/ppermute | solution.py:364
  20.0 4.7 %collective-permute-start.9 = (bf16[16,2048]{1,0:T(8,128)(2,1)S(1)}, bf16[16,2048]{1,0:T(8,128)(2,1)S(1)}, u32[]{:S(2)}, u32[]{:S(2)}) collective-permute-start(bf16[16,2048]{1,0:T(8,128)(2,1)S(1)} %collective-permute-done.8.refs_3_), channel_id=1, source_target_pairs={{0,16},{16,0},{1,17},{17,1},{2,18},{18,2},{3,19},{19,3},{4,20},{20... | collective-permute-start | bytes 196616 | tf_op jit(solution)/shard_map/ppermute | solution.py:364
  24.6 1.5 %collective-permute-start.13 = (bf16[2,16,1024]{2,1,0:T(8,128)(2,1)S(1)}, bf16[2,16,1024]{2,1,0:T(8,128)(2,1)S(1)}, u32[]{:S(2)}, u32[]{:S(2)}) collective-permute-start(bf16[2,16,1024]{2,1,0:T(8,128)(2,1)S(1)} %get-tuple-element.34), channel_id=1, source_target_pairs={{0,1},{1,0},{2,3},{3,2},{4,5},{5,4},{6,7},{7,6},{8,9},{9,8},{10,11... | collective-permute-start | bytes 196616 | tf_op jit(solution)/shard_map/ppermute | solution.py:364
  25.5 2.1 %collective-permute-start.10 = (bf16[2,16,1024]{2,1,0:T(8,128)(2,1)S(1)}, bf16[2,16,1024]{2,1,0:T(8,128)(2,1)S(1)}, u32[]{:S(2)}, u32[]{:S(2)}) collective-permute-start(bf16[2,16,1024]{2,1,0:T(8,128)(2,1)S(1)} %get-tuple-element.32), channel_id=1, source_target_pairs={{0,1},{1,0},{2,3},{3,2},{4,5},{5,4},{6,7},{7,6},{8,9},{9,8},{10,11... | collective-permute-start | bytes 196616 | tf_op jit(solution)/shard_map/ppermute | solution.py:364
  26.1 4.0 %collective-permute-start.14 = (bf16[16,1024]{1,0:T(8,128)(2,1)S(1)}, bf16[16,1024]{1,0:T(8,128)(2,1)S(1)}, u32[]{:S(2)}, u32[]{:S(2)}) collective-permute-start(bf16[16,1024]{1,0:T(8,128)(2,1)S(1)} %fusion.3), channel_id=1, source_target_pairs={{0,2},{1,3},{2,0},{3,1},{16,18},{17,19},{18,16},{19,17},{4,6},{5,7... | collective-permute-start | bytes 98312 | tf_op jit(solution)/shard_map/ppermute | solution.py:364
  27.7 4.9 %collective-permute-start.12 = (bf16[16,1024]{1,0:T(8,128)(2,1)S(1)}, bf16[16,1024]{1,0:T(8,128)(2,1)S(1)}, u32[]{:S(2)}, u32[]{:S(2)}) collective-permute-start(bf16[16,1024]{1,0:T(8,128)(2,1)S(1)} %get-tuple-element.38), channel_id=1, source_target_pairs={{0,18},{1,19},{2,16},{3,17},{16,2},{17,3},{18,0},{19,1},{4,22},{5,... | collective-permute-start | bytes 98312 | tf_op jit(solution)/shard_map/ppermute | solution.py:364
  29.0 4.0 %collective-permute-start.11 = (bf16[16,1024]{1,0:T(8,128)(2,1)S(1)}, bf16[16,1024]{1,0:T(8,128)(2,1)S(1)}, u32[]{:S(2)}, u32[]{:S(2)}) collective-permute-start(bf16[16,1024]{1,0:T(8,128)(2,1)S(1)} %get-tuple-element.37), channel_id=1, source_target_pairs={{0,16},{1,17},{2,18},{3,19},{16,0},{17,1},{18,2},{19,3},{4,20},{5,... | collective-permute-start | bytes 98312 | tf_op jit(solution)/shard_map/ppermute | solution.py:364

commit v2 on v1

--- a/solution.py
+++ b/solution.py
@@ -387,17 +387,22 @@
     attended = final_merge(own, stat, arrived, heads)
 
     weight = fetch(attended, out_weight)
-    line = [attended]
+    plane, n = ("group", "tensor"), groups * tensor
+    crossed = [attended]
+    for kg in range(1, groups):
+        crossed.append(swap(attended, "group", groups, kg))
+    columns = [[b] + [None] * (dps - 1) for b in crossed]
     for k in range(1, dps):
-        line.append(swap(attended, "dp", dps, k))
-    plane, n = ("group", "tensor"), groups * tensor
+        if k == 1:
+            got = swap(jnp.stack(crossed), "dp", dps, k)
+            for kg in range(groups):
+                columns[kg][k] = got[kg]
+            continue
+        columns[0][k] = swap(attended, "dp", dps, k)
+        for kg in range(1, groups):
+            columns[kg][k] = swap(columns[0][k], "group", groups, kg)
     sums = []
-    for kg in range(groups):
-        blocks = line
-        if kg:
-            blocks = []
-            for b in line:
-                blocks.append(swap(b, "group", groups, kg))
+    for kg, blocks in enumerate(columns):
         send, keep = project(blocks, weight)
         both = keep + swap(send, "tensor", tensor, 1).astype(F32)
         total = 0.0 if kg else both[0]

time: 33.8 us -> 38.1 us (1.13)
  waiting for transfers between devices: 6.87 us -> 11.5 us
    ppermute x15 -> x14, waiting for transfers between devices: 6.87 us -> 11.5 us  [swap(): return lax.ppermute(x, axes, [(i, i ^ k) for i in range(n)])]
    ppermute x15 -> x14, starting transfers between devices: 18.1 us -> 17.8 us  [swap(): return lax.ppermute(x, axes, [(i, i ^ k) for i in range(n)])]
  transfers between devices with their start and end apart: 15 -> 14, of which waited for: 6 -> 7; matrix products, arithmetic and copies ran while one was open for 0% -> 0% of each run, Pallas kernels for 17% -> 15%
where the time goes in v2:
time: 38.1 us; the launch traced here: 38 us
  starting transfers between devices  17.8 us (47%)
  waiting for transfers between devices  11.5 us (30%)
  Pallas kernels  7.78 us (20%)
  local copies, waits for them, and re-layouts  0.72 us (2%)
    ppermute x14, starting transfers between devices, swap(): return lax.ppermute(x, axes, [(i, i ^ k) for i in range(n)])  17.8 us
    ppermute x14, waiting for transfers between devices, swap(): return lax.ppermute(x, axes, [(i, i ^ k) for i in range(n)])  11.5 us
    pallas_call x1, Pallas kernels, fetch(): pl.pallas_call(fetch_kernel, out_shape=vmem(weight.shape, weight.dtype),...  2.2 us
    pallas_call x1, Pallas kernels, first(): pl.pallas_call(functools.partial(first_kernel, self.heads, self.join, chu...  1.74 us
    pallas_call x2, Pallas kernels, project(): pl.pallas_call(functools.partial(project_kernel, n), out_shape=(vmem(shap...  1.69 us
    pallas_call x2, Pallas kernels, keep(): pl.pallas_call(functools.partial(keep_kernel, self.heads, self.join, chun...  0.91 us
  transfers between devices with their start and end apart: 14, of which 7 were waited for; matrix products, arithmetic and copies ran while one was open for 0% of the time, Pallas kernels for 15%

profile of v2, /device:TPU:0, one launch (start us, length us, event | category | flops | bytes accessed | tf_op | source)
XLA Modules:
  0.0 38.0 jit_solution(7282766118073474447)
XLA Ops:
  0.0 1.7 %attend_first.1 = (bf16[1,16,2176]{2,1,0:T(8,128)(2,1)S(1)}, bf16[4,4,4,2048]{3,2,1,0:T(4,128)(2,1)S(1)}, bf16[4,4,2,128,128]{4,3,2,1,0:T(8,128)(2,1)S(1)}, bf16...) custom-call(s32[4]{0:T(128)} %len_hbm.1, bf16[4,4,8192]{2,1,0:T(4,128)(2,1)} %q_hbm.1, ...), custom_call_target="tpu_custom_call" | custom-call | flops 67108864 | tf_op jit(solution)/shard_map/attend_first/pallas_call | solution.py:207
  1.7 0.6 %collective-permute-start.1 = (bf16[1,16,2176]{2,1,0:T(8,128)(2,1)S(1)}, bf16[1,16,2176]{2,1,0:T(8,128)(2,1)S(1)}, u32[]{:S(2)}, u32[]{:S(2)}) collective-permute-start(bf16[1,16,2176]{2,1,0:T(8,128)(2,1)S(1)} %get-tuple-element.30), channel_id=1, source_target_pairs={{0,1},{1,0},{2,3},{3,2},{4,5},{5,4},{6,7},{7,6},{8,9},{9,8},{10,11... | collective-permute-start | bytes 208904 | tf_op jit(solution)/shard_map/ppermute | solution.py:364
  2.3 0.5 %attend_send.1 = bf16[16,2176]{1,0:T(8,128)(2,1)S(1)} custom-call(bf16[4,4,4,2048]{3,2,1,0:T(4,128)(2,1)S(1)} %get-tuple-element.20.q_ref, bf16[4,4,2,128,128]{4,3,2,1,0:T(8,128)(2,1)S(1)} %get-tuple-element.21.k_ref, bf16[4,4,2,128,128]{4,3,2,1,0:T(8,128)(2,1)S(1)} %get-tuple-element.22.v_ref, s32[4,32,128]{2,1,0:T(8,128)S(1)} %get-tuple-element.23.gap_ref), custom_call_target="tpu_custom_call" | custom-call | flops 67108864 | tf_op jit(solution)/shard_map/attend_send/pallas_call | solution.py:224
  2.8 0.0 collective-permute-start
  2.9 0.5 %attend_keep.3 = (f32[1,16,2048]{2,1,0:T(8,128)S(1)}, f32[1,2,16,128]{3,2,1,0:T(8,128)S(1)}) custom-call(bf16[4,4,4,2048]{3,2,1,0:T(4,128)(2,1)S(1)} %get-tuple-element.20.q_ref, bf16[4,4,2,128,128]{4,3,2,1,0:T(8,128)(2,1)S(1)} %get-tuple-element.21.k_ref, bf16[4,4,2,128,128]{4,3,2,1,0:T(8,128)(2,1)S(1)} %get-tuple-element.22.v_ref, ...), custom_call_target="tpu_custom_call" | custom-call | flops 67108864 | tf_op jit(solution)/shard_map/attend_keep/pallas_call | solution.py:236
  3.3 0.0 collective-permute-done.1.recv_ref
  3.3 0.2 core_merge.1
  3.6 3.0 %collective-permute-start.2 = (bf16[16,2176]{1,0:T(8,128)(2,1)S(1)}, bf16[16,2176]{1,0:T(8,128)(2,1)S(1)}, u32[]{:S(2)}, u32[]{:S(2)}) collective-permute-start(bf16[16,2176]{1,0:T(8,128)(2,1)S(1)} %bitcast.31), channel_id=1, source_target_pairs={{0,2},{1,3},{2,0},{3,1},{4,6},{5,7},{6,4},{7,5},{8,10},{9,11},{10,... | collective-permute-start | bytes 208904 | tf_op jit(solution)/shard_map/ppermute | solution.py:364
  6.6 0.5 %attend_keep.2 = (f32[1,16,2048]{2,1,0:T(8,128)S(1)}, f32[1,2,16,128]{3,2,1,0:T(8,128)S(1)}) custom-call(bf16[4,4,4,2048]{3,2,1,0:T(4,128)(2,1)S(1)} %get-tuple-element.20.q_ref, bf16[4,4,2,128,128]{4,3,2,1,0:T(8,128)(2,1)S(1)} %get-tuple-element.21.k_ref, bf16[4,4,2,128,128]{4,3,2,1,0:T(8,128)(2,1)S(1)} %get-tuple-element.22.v_ref, ...), custom_call_target="tpu_custom_call" | custom-call | flops 67108864 | tf_op jit(solution)/shard_map/attend_keep/pallas_call | solution.py:236
  7.1 0.0 collective-permute-done.recv_ref
  7.1 0.2 near_merge.1
  7.3 1.7 %collective-permute-done.2.refs_0_ = bf16[16,2176]{1,0:T(8,128)(2,1)S(1)} collective-permute-done((bf16[16,2176]{1,0:T(8,128)(2,1)S(1)}, bf16[16,2176]{1,0:T(8,128)(2,1)S(1)}, u32[]{:S(2)}, u32[]{:S(2)}) %collective-permute-start.2) | collective-permute-done | bytes 69664 | tf_op jit(solution)/shard_map/ppermute | solution.py:364
  9.0 0.2 final_merge.1._.refs_0_
  9.2 2.0 %collective-permute-start.3 = (bf16[16,2048]{1,0:T(8,128)(2,1)S(1)}, bf16[16,2048]{1,0:T(8,128)(2,1)S(1)}, u32[]{:S(2)}, u32[]{:S(2)}) collective-permute-start(bf16[16,2048]{1,0:T(8,128)(2,1)S(1)} %final_merge.1._.refs_0_), channel_id=1, source_target_pairs={{0,16},{16,0},{1,17},{17,1},{2,18},{18,2},{3,19},{19,3},{4,20},{20... | collective-permute-start | bytes 196616 | tf_op jit(solution)/shard_map/ppermute | solution.py:364
  11.3 2.3 %collective-permute-done.3.refs_0_ = bf16[16,2048]{1,0:T(8,128)(2,1)S(1)} collective-permute-done((bf16[16,2048]{1,0:T(8,128)(2,1)S(1)}, bf16[16,2048]{1,0:T(8,128)(2,1)S(1)}, u32[]{:S(2)}, u32[]{:S(2)}) %collective-permute-start.3) | collective-permute-done | bytes 65568 | tf_op jit(solution)/shard_map/ppermute | solution.py:364
  13.6 2.1 %collective-permute-start.4 = (bf16[2,16,2048]{2,1,0:T(8,128)(2,1)S(1)}, bf16[2,16,2048]{2,1,0:T(8,128)(2,1)S(1)}, u32[]{:S(2)}, u32[]{:S(2)}) collective-permute-start(bf16[2,16,2048]{2,1,0:T(8,128)(2,1)S(1)} %pad_maximum_fusion), channel_id=1, source_target_pairs={{0,4},{4,0},{8,12},{12,8},{1,5},{5,1},{9,13},{13,9},{2,6},{6,2},{1... | collective-permute-start | bytes 393224 | tf_op jit(solution)/shard_map/ppermute | solution.py:364
  15.7 2.6 %collective-permute-start.5 = (bf16[16,2048]{1,0:T(8,128)(2,1)S(1)}, bf16[16,2048]{1,0:T(8,128)(2,1)S(1)}, u32[]{:S(2)}, u32[]{:S(2)}) collective-permute-start(bf16[16,2048]{1,0:T(8,128)(2,1)S(1)} %final_merge.1._.refs_0_), channel_id=1, source_target_pairs={{0,8},{4,12},{8,0},{12,4},{1,9},{5,13},{9,1},{13,5},{2,10},{6,14},... | collective-permute-start | bytes 196616 | tf_op jit(solution)/shard_map/ppermute | solution.py:364
  18.3 0.0 collective-permute-start.7
  18.3 2.2 %fetch.1.refs_4_ = bf16[2048,1024]{1,0:T(8,128)(2,1)S(1)} custom-call(bf16[16,2048]{1,0:T(8,128)(2,1)S(1)} %final_merge.1._.refs_0_, bf16[2048,1024]{1,0:T(8,128)(2,1)} %w_hbm.1), custom_call_target="tpu_custom_call" | custom-call | flops 134217728 | bytes 4194304 | tf_op jit(solution)/shard_map/fetch/pallas_call | solution.py:41
  20.5 0.9 %collective-permute-done.5.refs_2_ = bf16[16,2048]{1,0:T(8,128)(2,1)S(1)} collective-permute-done((bf16[16,2048]{1,0:T(8,128)(2,1)S(1)}, bf16[16,2048]{1,0:T(8,128)(2,1)S(1)}, u32[]{:S(2)}, u32[]{:S(2)}) %collective-permute-start.5) | collective-permute-done | bytes 65568 | tf_op jit(solution)/shard_map/ppermute | solution.py:364
  21.4 1.5 %collective-permute-start.6 = (bf16[16,2048]{1,0:T(8,128)(2,1)S(1)}, bf16[16,2048]{1,0:T(8,128)(2,1)S(1)}, u32[]{:S(2)}, u32[]{:S(2)}) collective-permute-start(bf16[16,2048]{1,0:T(8,128)(2,1)S(1)} %collective-permute-done.5.refs_2_), channel_id=1, source_target_pairs={{0,16},{16,0},{1,17},{17,1},{2,18},{18,2},{3,19},{19,3},{4,20},{20... | collective-permute-start | bytes 196616 | tf_op jit(solution)/shard_map/ppermute | solution.py:364
  22.9 1.4 %collective-permute-done.7.refs_3_ = bf16[16,2048]{1,0:T(8,128)(2,1)S(1)} collective-permute-done((bf16[16,2048]{1,0:T(8,128)(2,1)S(1)}, bf16[16,2048]{1,0:T(8,128)(2,1)S(1)}, u32[]{:S(2)}, u32[]{:S(2)}) %collective-permute-start.7) | collective-permute-done | bytes 65568 | tf_op jit(solution)/shard_map/ppermute | solution.py:364
  24.3 1.5 %collective-permute-start.8 = (bf16[16,2048]{1,0:T(8,128)(2,1)S(1)}, bf16[16,2048]{1,0:T(8,128)(2,1)S(1)}, u32[]{:S(2)}, u32[]{:S(2)}) collective-permute-start(bf16[16,2048]{1,0:T(8,128)(2,1)S(1)} %collective-permute-done.7.refs_3_), channel_id=1, source_target_pairs={{0,16},{16,0},{1,17},{17,1},{2,18},{18,2},{3,19},{19,3},{4,20},{20... | collective-permute-start | bytes 196616 | tf_op jit(solution)/shard_map/ppermute | solution.py:364
  25.8 0.0 collective-permute-done.4
  25.9 0.8 %project.3 = (bf16[2,16,1024]{2,1,0:T(8,128)(2,1)S(1)}, f32[2,16,1024]{2,1,0:T(8,128)S(1)}) custom-call(bf16[16,2048]{1,0:T(8,128)(2,1)S(1)} %final_merge.1._.refs_0_, bf16[16,2048]{1,0:T(8,128)(2,1)S(1)} %get-tuple-element.38.refs_1_, bf16[16,2048]{1,0:T(8,128)(2,1)S(1)} %collective-permute-done.5.refs_2_, ...), custom_call_target="tpu_custom_call" | custom-call | flops 268435456 | tf_op jit(solution)/shard_map/project/pallas_call | solution.py:351
  26.7 0.1 collective-permute-start.12
  26.8 0.0 collective-permute-done.6.refs_2_
  26.8 1.8 %collective-permute-done.8.refs_3_ = bf16[16,2048]{1,0:T(8,128)(2,1)S(1)} collective-permute-done((bf16[16,2048]{1,0:T(8,128)(2,1)S(1)}, bf16[16,2048]{1,0:T(8,128)(2,1)S(1)}, u32[]{:S(2)}, u32[]{:S(2)}) %collective-permute-start.8) | collective-permute-done | bytes 65568 | tf_op jit(solution)/shard_map/ppermute | solution.py:364
  28.6 0.8 %project.2 = (bf16[2,16,1024]{2,1,0:T(8,128)(2,1)S(1)}, f32[2,16,1024]{2,1,0:T(8,128)S(1)}) custom-call(bf16[16,2048]{1,0:T(8,128)(2,1)S(1)} %collective-permute-done.3.refs_0_, bf16[16,2048]{1,0:T(8,128)(2,1)S(1)} %get-tuple-element.37.refs_1_, bf16[16,2048]{1,0:T(8,128)(2,1)S(1)} %collective-permute-done.6.refs_2_, ...), custom_call_target="tpu_custom_call" | custom-call | flops 268435456 | tf_op jit(solution)/shard_map/project/pallas_call | solution.py:351
  29.4 0.1 collective-permute-start.9
  29.5 0.0 collective-permute-done.12
  29.6 1.6 %collective-permute-start.13 = (bf16[16,1024]{1,0:T(8,128)(2,1)S(1)}, bf16[16,1024]{1,0:T(8,128)(2,1)S(1)}, u32[]{:S(2)}, u32[]{:S(2)}) collective-permute-start(bf16[16,1024]{1,0:T(8,128)(2,1)S(1)} %fusion.3), channel_id=1, source_target_pairs={{0,2},{1,3},{2,0},{3,1},{16,18},{17,19},{18,16},{19,17},{4,6},{5,7... | collective-permute-start | bytes 98312 | tf_op jit(solution)/shard_map/ppermute | solution.py:364
  31.1 0.0 collective-permute-done.9
  31.2 2.1 %collective-permute-start.11 = (bf16[16,1024]{1,0:T(8,128)(2,1)S(1)}, bf16[16,1024]{1,0:T(8,128)(2,1)S(1)}, u32[]{:S(2)}, u32[]{:S(2)}) collective-permute-start(bf16[16,1024]{1,0:T(8,128)(2,1)S(1)} %get-tuple-element.40), channel_id=1, source_target_pairs={{0,18},{1,19},{2,16},{3,17},{16,2},{17,3},{18,0},{19,1},{4,22},{5,... | collective-permute-start | bytes 98312 | tf_op jit(solution)/shard_map/ppermute | solution.py:364
  33.3 0.5 %collective-permute-start.10 = (bf16[16,1024]{1,0:T(8,128)(2,1)S(1)}, bf16[16,1024]{1,0:T(8,128)(2,1)S(1)}, u32[]{:S(2)}, u32[]{:S(2)}) collective-permute-start(bf16[16,1024]{1,0:T(8,128)(2,1)S(1)} %get-tuple-element.39), channel_id=1, source_target_pairs={{0,16},{1,17},{2,18},{3,19},{16,0},{17,1},{18,2},{19,3},{4,20},{5,... | collective-permute-start | bytes 98312 | tf_op jit(solution)/shard_map/ppermute | solution.py:364
  33.8 0.0 collective-permute-done.13
  33.8 2.3 %collective-permute-done.11 = bf16[16,1024]{1,0:T(8,128)(2,1)S(1)} collective-permute-done((bf16[16,1024]{1,0:T(8,128)(2,1)S(1)}, bf16[16,1024]{1,0:T(8,128)(2,1)S(1)}, u32[]{:S(2)}, u32[]{:S(2)}) %collective-permute-start.11) | collective-permute-done | bytes 32800 | tf_op jit(solution)/shard_map/ppermute | solution.py:364
  36.1 1.2 %collective-permute-done.10 = bf16[16,1024]{1,0:T(8,128)(2,1)S(1)} collective-permute-done((bf16[16,1024]{1,0:T(8,128)(2,1)S(1)}, bf16[16,1024]{1,0:T(8,128)(2,1)S(1)}, u32[]{:S(2)}, u32[]{:S(2)}) %collective-permute-start.10) | collective-permute-done | bytes 32800 | tf_op jit(solution)/shard_map/ppermute | solution.py:364
  37.3 0.7 %copy.6 = bf16[16,2,1024]{2,1,0:T(2,128)(2,1)} copy(bf16[16,2,1024]{2,0,1:T(8,128)(2,1)S(1)} %pad_maximum_fusion.1) | data formatting | bytes 131072 | tf_op jit(solution)/shard_map/stack | solution.py:420
  (8 shorter events, 0.1 us)
Async XLA Ops:
  1.7 1.6 %collective-permute-start.1 = (bf16[1,16,2176]{2,1,0:T(8,128)(2,1)S(1)}, bf16[1,16,2176]{2,1,0:T(8,128)(2,1)S(1)}, u32[]{:S(2)}, u32[]{:S(2)}) collective-permute-start(bf16[1,16,2176]{2,1,0:T(8,128)(2,1)S(1)} %get-tuple-element.30), channel_id=1, source_target_pairs={{0,1},{1,0},{2,3},{3,2},{4,5},{5,4},{6,7},{7,6},{8,9},{9,8},{10,11... | collective-permute-start | bytes 208904 | tf_op jit(solution)/shard_map/ppermute | solution.py:364
  2.8 4.2 %collective-permute-start = (bf16[16,2176]{1,0:T(8,128)(2,1)S(1)}, bf16[16,2176]{1,0:T(8,128)(2,1)S(1)}, u32[]{:S(2)}, u32[]{:S(2)}) collective-permute-start(bf16[16,2176]{1,0:T(8,128)(2,1)S(1)} %attend_send.1), channel_id=1, source_target_pairs={{0,1},{1,0},{2,3},{3,2},{4,5},{5,4},{6,7},{7,6},{8,9},{9,8},{10,11... | collective-permute-start | bytes 208904 | tf_op jit(solution)/shard_map/ppermute | solution.py:364
  3.6 5.4 %collective-permute-start.2 = (bf16[16,2176]{1,0:T(8,128)(2,1)S(1)}, bf16[16,2176]{1,0:T(8,128)(2,1)S(1)}, u32[]{:S(2)}, u32[]{:S(2)}) collective-permute-start(bf16[16,2176]{1,0:T(8,128)(2,1)S(1)} %bitcast.31), channel_id=1, source_target_pairs={{0,2},{1,3},{2,0},{3,1},{4,6},{5,7},{6,4},{7,5},{8,10},{9,11},{10,... | collective-permute-start | bytes 208904 | tf_op jit(solution)/shard_map/ppermute | solution.py:364
  9.2 4.3 %collective-permute-start.3 = (bf16[16,2048]{1,0:T(8,128)(2,1)S(1)}, bf16[16,2048]{1,0:T(8,128)(2,1)S(1)}, u32[]{:S(2)}, u32[]{:S(2)}) collective-permute-start(bf16[16,2048]{1,0:T(8,128)(2,1)S(1)} %final_merge.1._.refs_0_), channel_id=1, source_target_pairs={{0,16},{16,0},{1,17},{17,1},{2,18},{18,2},{3,19},{19,3},{4,20},{20... | collective-permute-start | bytes 196616 | tf_op jit(solution)/shard_map/ppermute | solution.py:364
  13.6 12.3 %collective-permute-start.4 = (bf16[2,16,2048]{2,1,0:T(8,128)(2,1)S(1)}, bf16[2,16,2048]{2,1,0:T(8,128)(2,1)S(1)}, u32[]{:S(2)}, u32[]{:S(2)}) collective-permute-start(bf16[2,16,2048]{2,1,0:T(8,128)(2,1)S(1)} %pad_maximum_fusion), channel_id=1, source_target_pairs={{0,4},{4,0},{8,12},{12,8},{1,5},{5,1},{9,13},{13,9},{2,6},{6,2},{1... | collective-permute-start | bytes 393224 | tf_op jit(solution)/shard_map/ppermute | solution.py:364
  15.7 5.7 %collective-permute-start.5 = (bf16[16,2048]{1,0:T(8,128)(2,1)S(1)}, bf16[16,2048]{1,0:T(8,128)(2,1)S(1)}, u32[]{:S(2)}, u32[]{:S(2)}) collective-permute-start(bf16[16,2048]{1,0:T(8,128)(2,1)S(1)} %final_merge.1._.refs_0_), channel_id=1, source_target_pairs={{0,8},{4,12},{8,0},{12,4},{1,9},{5,13},{9,1},{13,5},{2,10},{6,14},... | collective-permute-start | bytes 196616 | tf_op jit(solution)/shard_map/ppermute | solution.py:364
  18.3 6.1 %collective-permute-start.7 = (bf16[16,2048]{1,0:T(8,128)(2,1)S(1)}, bf16[16,2048]{1,0:T(8,128)(2,1)S(1)}, u32[]{:S(2)}, u32[]{:S(2)}) collective-permute-start(bf16[16,2048]{1,0:T(8,128)(2,1)S(1)} %final_merge.1._.refs_0_), channel_id=1, source_target_pairs={{0,12},{4,8},{8,4},{12,0},{1,13},{5,9},{9,5},{13,1},{2,14},{6,10},... | collective-permute-start | bytes 196616 | tf_op jit(solution)/shard_map/ppermute | solution.py:364
  21.4 5.4 %collective-permute-start.6 = (bf16[16,2048]{1,0:T(8,128)(2,1)S(1)}, bf16[16,2048]{1,0:T(8,128)(2,1)S(1)}, u32[]{:S(2)}, u32[]{:S(2)}) collective-permute-start(bf16[16,2048]{1,0:T(8,128)(2,1)S(1)} %collective-permute-done.5.refs_2_), channel_id=1, source_target_pairs={{0,16},{16,0},{1,17},{17,1},{2,18},{18,2},{3,19},{19,3},{4,20},{20... | collective-permute-start | bytes 196616 | tf_op jit(solution)/shard_map/ppermute | solution.py:364
  24.3 4.3 %collective-permute-start.8 = (bf16[16,2048]{1,0:T(8,128)(2,1)S(1)}, bf16[16,2048]{1,0:T(8,128)(2,1)S(1)}, u32[]{:S(2)}, u32[]{:S(2)}) collective-permute-start(bf16[16,2048]{1,0:T(8,128)(2,1)S(1)} %collective-permute-done.7.refs_3_), channel_id=1, source_target_pairs={{0,16},{16,0},{1,17},{17,1},{2,18},{18,2},{3,19},{19,3},{4,20},{20... | collective-permute-start | bytes 196616 | tf_op jit(solution)/shard_map/ppermute | solution.py:364
  26.7 2.8 %collective-permute-start.12 = (bf16[2,16,1024]{2,1,0:T(8,128)(2,1)S(1)}, bf16[2,16,1024]{2,1,0:T(8,128)(2,1)S(1)}, u32[]{:S(2)}, u32[]{:S(2)}) collective-permute-start(bf16[2,16,1024]{2,1,0:T(8,128)(2,1)S(1)} %get-tuple-element.34), channel_id=1, source_target_pairs={{0,1},{1,0},{2,3},{3,2},{4,5},{5,4},{6,7},{7,6},{8,9},{9,8},{10,11... | collective-permute-start | bytes 196616 | tf_op jit(solution)/shard_map/ppermute | solution.py:364
  29.4 1.7 %collective-permute-start.9 = (bf16[2,16,1024]{2,1,0:T(8,128)(2,1)S(1)}, bf16[2,16,1024]{2,1,0:T(8,128)(2,1)S(1)}, u32[]{:S(2)}, u32[]{:S(2)}) collective-permute-start(bf16[2,16,1024]{2,1,0:T(8,128)(2,1)S(1)} %get-tuple-element.32), channel_id=1, source_target_pairs={{0,1},{1,0},{2,3},{3,2},{4,5},{5,4},{6,7},{7,6},{8,9},{9,8},{10,11... | collective-permute-start | bytes 196616 | tf_op jit(solution)/shard_map/ppermute | solution.py:364
  29.6 4.3 %collective-permute-start.13 = (bf16[16,1024]{1,0:T(8,128)(2,1)S(1)}, bf16[16,1024]{1,0:T(8,128)(2,1)S(1)}, u32[]{:S(2)}, u32[]{:S(2)}) collective-permute-start(bf16[16,1024]{1,0:T(8,128)(2,1)S(1)} %fusion.3), channel_id=1, source_target_pairs={{0,2},{1,3},{2,0},{3,1},{16,18},{17,19},{18,16},{19,17},{4,6},{5,7... | collective-permute-start | bytes 98312 | tf_op jit(solution)/shard_map/ppermute | solution.py:364
  31.2 4.9 %collective-permute-start.11 = (bf16[16,1024]{1,0:T(8,128)(2,1)S(1)}, bf16[16,1024]{1,0:T(8,128)(2,1)S(1)}, u32[]{:S(2)}, u32[]{:S(2)}) collective-permute-start(bf16[16,1024]{1,0:T(8,128)(2,1)S(1)} %get-tuple-element.40), channel_id=1, source_target_pairs={{0,18},{1,19},{2,16},{3,17},{16,2},{17,3},{18,0},{19,1},{4,22},{5,... | collective-permute-start | bytes 98312 | tf_op jit(solution)/shard_map/ppermute | solution.py:364
  33.3 3.9 %collective-permute-start.10 = (bf16[16,1024]{1,0:T(8,128)(2,1)S(1)}, bf16[16,1024]{1,0:T(8,128)(2,1)S(1)}, u32[]{:S(2)}, u32[]{:S(2)}) collective-permute-start(bf16[16,1024]{1,0:T(8,128)(2,1)S(1)} %get-tuple-element.39), channel_id=1, source_target_pairs={{0,16},{1,17},{2,18},{3,19},{16,0},{17,1},{18,2},{19,3},{4,20},{5,... | collective-permute-start | bytes 98312 | tf_op jit(solution)/shard_map/ppermute | solution.py:364
